TPU v7x, 32 devices: a 4x4x1 block of a 4x4x8 slice. The times are simulated.
32 devices in a mesh: replica: 1 (over z), yz: 4 (over y), x: 8 (over x, core).
Axes of the slice: x: 4, y: 4, z: 1, core: 2. Of those that a mesh axis runs over, the one named last changes fastest.
The devices are a block of a 4x4x8 slice.
Arguments:
- hidden: bfloat16 [512, 1536], P('replica', ('x', 'yz'))
- seq_lens: int32 [512], P(('replica', 'yz', 'x'))
- attn_gain: bfloat16 [1, 1536], replicated
- mlp_gain: bfloat16 [1, 1536], replicated
- w_qkv: bfloat16 [1, 1536, 1792], P(None, None, 'yz')
- w_out: bfloat16 [1, 1536, 1536], P(None, 'yz')
- w_gate_up: bfloat16 [1, 1536, 2, 8960], P(None, None, None, 'yz')
- w_down: bfloat16 [1, 8960, 1536], P(None, 'yz')
- k_cache: bfloat16 [1, 512, 2048, 128], P(None, ('replica', 'yz', 'x'))
- v_cache: bfloat16 [1, 512, 2048, 128], P(None, ('replica', 'yz', 'x'))
Outputs:
- output 1: bfloat16 [512, 1536], P('replica', ('x', 'yz'))
- output 2: bfloat16 [1, 512, 2048, 128], P(None, ('replica', 'yz', 'x'))
- output 3: bfloat16 [1, 512, 2048, 128], P(None, ('replica', 'yz', 'x'))
All inputs are finite; a program needn't handle non-finite values.
Results may differ from a plain program's by a relative error of at most 0.0155586.
Values are sent between devices in bfloat16 or wider.
A program may use at most 768 MiB of HBM per device.

v0:
```python
import jax
import jax.numpy as jnp
from jax import lax
from jax.sharding import PartitionSpec as P

NORM_EPS = 1e-5


def attend(z_rows, k_layer, v_layer, seq_lens, head_dim):
    num_rows = z_rows.shape[0]
    attn_width = z_rows.shape[1] - 2 * head_dim
    num_heads = attn_width // head_dim
    queries = z_rows[:, :attn_width].reshape(num_rows, num_heads, head_dim)
    k_new = z_rows[:, attn_width:attn_width + head_dim]
    v_new = z_rows[:, attn_width + head_dim:]
    slot_ids = jnp.arange(k_layer.shape[1])
    at_slot = (slot_ids[None, :] == seq_lens[:, None])[:, :, None]
    k_upd = jnp.where(at_slot, k_new[:, None, :], k_layer)
    v_upd = jnp.where(at_slot, v_new[:, None, :], v_layer)
    scores = jnp.einsum('bhd,bsd->bhs', queries, k_upd, preferred_element_type=jnp.float32) * head_dim ** -0.5
    visible = (slot_ids[None, :] <= seq_lens[:, None])[:, None, :]
    scores = jnp.where(visible, scores, -1e30)
    probs_bf = jax.nn.softmax(scores, axis=-1).astype(jnp.bfloat16)
    outputs = jnp.einsum('bhs,bsd->bhd', probs_bf, v_upd, preferred_element_type=jnp.float32)
    return outputs.astype(jnp.bfloat16).reshape(num_rows, attn_width), k_upd, v_upd


def solution(mesh):
    group_axes = ('yz', 'x')
    batch_axes = ('replica', 'yz', 'x')
    hidden_spec = P('replica', ('x', 'yz'))
    cache_spec = P(None, batch_axes, None, None)
    x_size = mesh.shape['x']

    def norm_part(h_part, gain_part, model_dim):
        hid_f = h_part.astype(jnp.float32)
        sq_power = lax.psum(jnp.sum(hid_f * hid_f, axis=1, keepdims=True), 'x')
        inv_scale = lax.rsqrt(sq_power / model_dim + NORM_EPS)
        return (hid_f * inv_scale * gain_part.astype(jnp.float32)).astype(jnp.bfloat16)

    def residual(hidden, partial_sum):
        summed = lax.psum_scatter(partial_sum.astype(jnp.bfloat16), 'yz', scatter_dimension=1, tiled=True)
        return (hidden.astype(jnp.float32) + summed.astype(jnp.float32)).astype(jnp.bfloat16)

    def local_step(hidden, seq_lens, attn_gain, mlp_gain, w_qkv, w_out, w_gate_up, w_down, k_cache, v_cache):
        head_dim = k_cache.shape[-1]
        model_dim = attn_gain.shape[1] * x_size
        k_layers = []
        v_layers = []
        for layer_idx in range(w_qkv.shape[0]):
            gathered = lax.all_gather(hidden, 'yz', axis=1, tiled=True)
            normed = norm_part(gathered, attn_gain[layer_idx], model_dim)
            partial_z = jnp.dot(normed, w_qkv[layer_idx], preferred_element_type=jnp.float32).astype(jnp.bfloat16)
            z_cols = lax.psum_scatter(partial_z, 'x', scatter_dimension=1, tiled=True)
            z_rows = lax.all_to_all(z_cols, group_axes, 0, 1, tiled=True)
            attn_rows, k_upd, v_upd = attend(z_rows, k_cache[layer_idx], v_cache[layer_idx], seq_lens, head_dim)
            k_layers.append(k_upd)
            v_layers.append(v_upd)
            attn_cols = lax.all_to_all(attn_rows, group_axes, 1, 0, tiled=True)
            attn_slab = lax.all_gather(attn_cols, 'x', axis=1, tiled=True)
            hidden = residual(hidden, jnp.dot(attn_slab, w_out[layer_idx], preferred_element_type=jnp.float32))
            gathered = lax.all_gather(hidden, 'yz', axis=1, tiled=True)
            normed = norm_part(gathered, mlp_gain[layer_idx], model_dim)
            gu_part = jnp.einsum('be,etf->btf', normed, w_gate_up[layer_idx], preferred_element_type=jnp.float32).astype(jnp.bfloat16)
            gu_cols = lax.psum_scatter(gu_part, 'x', scatter_dimension=2, tiled=True)
            mlp_cols = (jax.nn.silu(gu_cols[:, 0].astype(jnp.float32)) * gu_cols[:, 1].astype(jnp.float32)).astype(jnp.bfloat16)
            mlp_slab = lax.all_gather(mlp_cols, 'x', axis=1, tiled=True)
            hidden = residual(hidden, jnp.dot(mlp_slab, w_down[layer_idx], preferred_element_type=jnp.float32))
        return hidden, jnp.stack(k_layers), jnp.stack(v_layers)

    return jax.shard_map(
        local_step,
        mesh=mesh,
        in_specs=(hidden_spec, P(batch_axes), P(None, 'x'), P(None, 'x'), P(None, 'x', 'yz'), P(None, 'yz', 'x'),
                  P(None, 'x', None, 'yz'), P(None, 'yz', 'x'), cache_spec, cache_spec),
        out_specs=(hidden_spec, cache_spec, cache_spec),
        check_vma=False)
```

profile of v0, /device:TPU:97, one launch (start us, length us, event | category | flops | bytes accessed | tf_op | source)
XLA Modules:
  0.0 294.0 jit_solution(4918130978637264319)
XLA Ops:
  7.2 0.1 reduce-scatter.7.cloned.1.call-start
  7.3 1.3 dynamic-slice.7
  8.6 1.2 dynamic-slice
  10.5 12.4 %all_gather.12 = bf16[512,192]{0,1:T(8,128)(2,1)S(1)} all-gather(bf16[512,48]{0,1:T(8,128)(2,1)} %param.10), channel_id=1, replica_groups=mesh['replica'=1,'yz'=4,'x'=8] {'yz'}, dimensions={1}, use_global_device_ids=true | all-gather | bytes 245760 | tf_op jit(solution)/shard_map/all_gather | solution.py:51
  22.9 0.1 fusion.22
  22.9 14.9 %psum.14 = f32[512,1]{0,1:T(1,128)S(1)} all-reduce(f32[512,1]{0,1:T(1,128)S(1)} %bitcast.74), channel_id=1, replica_groups=mesh['replica'=1,'yz'=4,'x'=8] {'x'}, use_global_device_ids=true, to_apply=%region_1.0 | all-reduce | flops 512 | bytes 4096 | tf_op jit(solution)/shard_map/psum | solution.py:37
  37.9 0.8 fusion.43
  38.7 1.8 convolution_convert_fusion.1
  40.5 25.2 %reduce-scatter.7.cloned.1.call-done = bf16[512,56]{0,1:T(8,128)(2,1)} async-done(((bf16[512,448]{0,1:T(8,128)(2,1)}), bf16[512,56]{0,1:T(8,128)(2,1)}) %reduce-scatter.7.cloned.1.call-update) | async-done | bytes 57360 | tf_op jit(solution)/shard_map/reduce_scatter | solution.py:54
  65.7 0.9 copy.18
  66.6 0.8 reshape.97
  67.5 6.8 %all-to-all-start = ((bf16[32,2,448]{2,1,0:T(2,128)(2,1)}), bf16[32,2,448]{2,1,0:T(2,128)(2,1)S(1)}, u32[]{:S(2)}, u32[]{:S(2)}) async-start(bf16[32,2,448]{2,1,0:T(2,128)(2,1)} %reshape.97), calls=%async_computation.1 | async-start | bytes 131072 | tf_op jit(solution)/shard_map/all_to_all | solution.py:55
  74.3 0.1 reduce-scatter.9.cloned.1.call-start
  74.4 0.8 iota_compare_fusion.1
  75.1 6.1 %all-to-all-done = bf16[32,2,448]{2,1,0:T(2,128)(2,1)S(1)} async-done(((bf16[32,2,448]{2,1,0:T(2,128)(2,1)}), bf16[32,2,448]{2,1,0:T(2,128)(2,1)S(1)}, u32[]{:S(2)}, u32[]{:S(2)}) %all-to-all-start) | async-done | bytes 57376 | tf_op jit(solution)/shard_map/all_to_all | solution.py:55
  81.2 0.2 reshape.98
  81.4 0.2 all_to_all.31
  81.7 10.4 %fusion.47 = (f32[16,12]{1,0:T(8,128)S(1)}, f32[16,12,2048]{2,1,0:T(8,128)}) fusion(bf16[16,12,128]{2,1,0:T(8,128)(2,1)S(1)} %reshape.81, bf16[1,16,2048,128]{3,2,1,0:T(8,128)(2,1)} %param.18, pred[16,2048]{1,0:T(8,128)(4,1)S(1)} %get-tuple-element.10, bf16[16,128]{1,0:T(8,128)(2,1)S(1)} %get-tuple-element.5, pred[16,2048]{1,0:T(8,128)(4,1)S(1)} %get-tuple-element.9), kind=kOutput, calls=%fused_computation.70 | convolution fusion | flops 106432512 | bytes 10081024 | tf_op jit(solution)/shard_map/sub | solution.py:23
  92.1 9.2 %fusion.15 = bf16[16,12,128]{2,1,0:T(8,128)(2,1)S(1)} fusion(bf16[1,16,2048,128]{3,2,1,0:T(8,128)(2,1)} %param.19, pred[16,2048]{1,0:T(8,128)(4,1)S(1)} %get-tuple-element.10, bf16[16,128]{1,0:T(8,128)(2,1)S(1)} %get-tuple-element.6, f32[16,12,2048]{2,1,0:T(8,128)} %get-tuple-element.12, f32[16,12]{1,0:T(8,128)S(1)} %get-tuple-element.11), kind=kOutput, calls=%fused_computation.24 | convolution fusion | flops 105668608 | bytes 10048256 | tf_op jit(solution)/shard_map/bhs,bsd->bhd/dot_general | solution.py:24
  101.3 0.2 all_to_all.32
  101.5 0.1 copy.35
  101.6 0.2 reshape.99
  101.8 9.7 %all_to_all.38 = bf16[32,2,384]{2,1,0:T(2,128)(2,1)S(1)} all-to-all(bf16[32,2,384]{2,1,0:T(2,128)(2,1)S(1)} %reshape.99), channel_id=1, replica_groups=mesh['replica'=1,'yz'=4,'x'=8] {'yz','x'}, dimensions={0} | all-to-all | bytes 98304 | tf_op jit(solution)/shard_map/all_to_all | solution.py:59
  111.5 0.2 reshape.100
  111.6 0.1 copy.21
  111.7 16.7 %all_gather.13 = bf16[512,384]{0,1:T(8,128)(2,1)S(1)} all-gather(bf16[512,48]{0,1:T(8,128)(2,1)S(1)} %copy.21), channel_id=1, replica_groups=mesh['replica'=1,'yz'=4,'x'=8] {'x'}, dimensions={1}, use_global_device_ids=true | all-gather | bytes 442368 | tf_op jit(solution)/shard_map/all_gather | solution.py:60
  128.5 2.7 convolution_convert_fusion.3
  131.2 0.1 reduce-scatter.13.cloned.1.call-start
  131.3 0.8 fusion.44
  132.1 19.0 %reduce-scatter.9.cloned.1.call-done = bf16[512,48]{0,1:T(8,128)(2,1)} async-done(((bf16[512,192]{0,1:T(8,128)(2,1)}), bf16[512,48]{0,1:T(8,128)(2,1)}) %reduce-scatter.9.cloned.1.call-update) | async-done | bytes 49168 | tf_op jit(solution)/shard_map/reduce_scatter | solution.py:42
  151.1 0.8 add_convert_fusion.1
  151.9 9.3 %all_gather.14 = bf16[512,192]{0,1:T(8,128)(2,1)S(1)} all-gather(bf16[512,48]{0,1:T(8,128)(2,1)S(1)} %add_convert_fusion.1), channel_id=1, replica_groups=mesh['replica'=1,'yz'=4,'x'=8] {'yz'}, dimensions={1}, use_global_device_ids=true | all-gather | bytes 245760 | tf_op jit(solution)/shard_map/all_gather | solution.py:62
  161.2 0.1 fusion.25
  161.3 17.7 %psum.15 = f32[512,1]{0,1:T(1,128)S(1)} all-reduce(f32[512,1]{0,1:T(1,128)S(1)} %bitcast.75), channel_id=1, replica_groups=mesh['replica'=1,'yz'=4,'x'=8] {'x'}, use_global_device_ids=true, to_apply=%region_7.8 | all-reduce | flops 512 | bytes 4096 | tf_op jit(solution)/shard_map/psum | solution.py:37
  179.0 4.1 %convolution_convert_fusion = bf16[512,2,2240]{0,2,1:T(8,128)(2,1)S(1)} fusion(bf16[1,1536,2,2240]{1,3,2,0:T(8,128)(2,1)} %param.16, s32[]{:T(128)} %bitcast.4, bf16[512,192]{0,1:T(8,128)(2,1)S(1)} %all_gather.14, f32[192]{0:T(256)S(1)} %bitcast.76, f32[512]{0:T(512)S(1)} %bitcast.73), kind=kOutput, calls=%fused_computation.9 | convolution fusion | flops 883490816 | bytes 7081216 | tf_op jit(solution)/shard_map/be,etf->btf/dot_general | solution.py:64
  183.0 17.9 %copy.23 = bf16[512,2,2240]{0,1,2:T(2,128)(2,1)S(1)} copy(bf16[512,2,2240]{0,2,1:T(8,128)(2,1)S(1)} %convolution_convert_fusion) | data formatting | bytes 9175040
  201.0 3.6 %copy.27 = bf16[280,8,2,512]{3,1,2,0:T(8,128)(2,1)} copy(bf16[280,8,2,512]{3,2,1,0:T(2,128)(2,1)S(1)} %bitcast.66) | data formatting | bytes 9175040
  204.6 0.2 all-gather.2.cloned.1.call-start
  204.9 30.8 %reduce-scatter.13.cloned.1.call-done = bf16[280,1024]{1,0:T(8,128)(2,1)} async-done(((bf16[2240,1024]{1,0:T(8,128)(2,1)}), bf16[280,1024]{1,0:T(8,128)(2,1)}) %reduce-scatter.13.cloned.1.call-update) | async-done | bytes 573456
  235.7 2.2 reshape.96
  237.8 0.8 fusion.45
  238.6 0.9 fusion.21
  239.6 0.1 reduce-scatter.11.cloned.1.call-start
  239.7 25.4 %all-gather.2.cloned.1.call-done = bf16[512,2240]{0,1:T(8,128)(2,1)} async-done(((bf16[512,280]{0,1:T(8,128)(2,1)}), bf16[512,2240]{0,1:T(8,128)(2,1)}) %all-gather.2.cloned.1.call-update) | async-done | bytes 2293776 | tf_op jit(solution)/shard_map/all_gather | solution.py:67
  265.0 4.7 %convolution_convert_fusion.2 = bf16[512,192]{0,1:T(8,128)(2,1)} fusion(bf16[512,2240]{0,1:T(8,128)(2,1)} %all-gather.2.cloned.1.call-done, bf16[1,2240,1536]{2,1,0:T(8,128)(2,1)} %param.17, s32[]{:T(128)} %bitcast.4), kind=kOutput, calls=%fused_computation.20 | convolution fusion | flops 440500224 | bytes 3637760 | tf_op jit(solution)/shard_map/dot_general | solution.py:68
  269.9 12.0 %broadcast_select_fusion = (bf16[1,16,2048,128]{3,2,1,0:T(8,128)(2,1)}, bf16[1,16,2048,128]{3,2,1,0:T(8,128)(2,1)}) fusion(bf16[1,16,2048,128]{3,2,1,0:T(8,128)(2,1)} %param.19, pred[16,2048]{1,0:T(8,128)(4,1)S(1)} %get-tuple-element.10, bf16[16,128]{1,0:T(8,128)(2,1)S(1)} %get-tuple-element.6, bf16[1,16,2048,128]{3,2,1,0:T(8,128)(2,1)} %param.18, ...), kind=kLoop, calls=%fused_computation.5 | loop fusion | flops 8388608 | bytes 33595392 | tf_op jit(solution)/shard_map/jit(_where)/select_n | solution.py:19
  281.8 4.2 %reduce-scatter.11.cloned.1.call-done = bf16[512,48]{0,1:T(8,128)(2,1)} async-done(((bf16[512,192]{0,1:T(8,128)(2,1)}), bf16[512,48]{0,1:T(8,128)(2,1)}) %reduce-scatter.11.cloned.1.call-update) | async-done | bytes 49168 | tf_op jit(solution)/shard_map/reduce_scatter | solution.py:42
  286.0 1.4 add_convert_fusion
  (17 shorter events, 0.4 us)
Async XLA Ops:
  7.2 31.5 %copy-start = (bf16[1,1536,448]{1,2,0:T(8,128)(2,1)S(1)}, bf16[1,1536,448]{1,2,0:T(8,128)(2,1)}, u32[]{:S(2)}) copy-start(bf16[1,1536,448]{1,2,0:T(8,128)(2,1)} %param.14) | copy-start | bytes 4128772
  7.2 58.5 %reduce-scatter.7.cloned.1.call-start = ((), (), s32[]{:S(2)}) async-start(), calls=%async_computation.6 | async-start | bytes 516096 | tf_op jit(solution)/shard_map/reduce_scatter | solution.py:54
  67.5 13.8 %all-to-all-start = ((bf16[32,2,448]{2,1,0:T(2,128)(2,1)}), bf16[32,2,448]{2,1,0:T(2,128)(2,1)S(1)}, u32[]{:S(2)}, u32[]{:S(2)}) async-start(bf16[32,2,448]{2,1,0:T(2,128)(2,1)} %reshape.97), calls=%async_computation.1 | async-start | bytes 131072 | tf_op jit(solution)/shard_map/all_to_all | solution.py:55
  74.3 76.8 %reduce-scatter.9.cloned.1.call-start = ((), (), s32[]{:S(2)}) async-start(), calls=%async_computation.7 | async-start | bytes 245760 | tf_op jit(solution)/shard_map/reduce_scatter | solution.py:42
  92.1 59.0 %copy-start.2 = (bf16[512,48]{0,1:T(8,128)(2,1)S(1)}, bf16[512,48]{0,1:T(8,128)(2,1)}, u32[]{:S(2)}) copy-start(bf16[512,48]{0,1:T(8,128)(2,1)} %param.10) | copy-start | bytes 147460
  131.2 104.4 %reduce-scatter.13.cloned.1.call-start = ((), (), s32[]{:S(2)}) async-start(), calls=%async_computation.10 | async-start | bytes 5160960
  204.6 60.4 %all-gather.2.cloned.1.call-start = ((), (), s32[]{:S(2)}) async-start(), calls=%async_computation.8 | async-start | bytes 2580480 | tf_op jit(solution)/shard_map/all_gather | solution.py:67
  239.6 46.4 %reduce-scatter.11.cloned.1.call-start = ((), (), s32[]{:S(2)}) async-start(), calls=%async_computation.9 | async-start | bytes 245760 | tf_op jit(solution)/shard_map/reduce_scatter | solution.py:42
  269.8 17.6 %copy-start.1 = (bf16[1,1536,448]{1,2,0:T(8,128)(2,1)S(1)}, bf16[1,1536,448]{1,2,0:T(8,128)(2,1)}, u32[]{:S(2)}) copy-start(bf16[1,1536,448]{1,2,0:T(8,128)(2,1)} %param.14) | copy-start | bytes 4128772
Sparse Core Ops, SparseCore 0:
  40.6 25.0 reduce-scatter.6
  131.4 19.6 reduce-scatter.8
  204.8 30.8 reduce-scatter.12
  239.7 25.2 all-gather.1
  270.0 15.9 reduce-scatter.10
where the time goes:
time: 296 us; the launch traced here: 294 us
  waiting for transfers between devices  111 us (38%)
  blocking collectives  80.7 us (27%)
  matrix products  32.9 us (11%)
  local copies, waits for them, and re-layouts  29.9 us (10%)
  other arithmetic  17.5 us (6%)
  between operations  14.6 us (5%)
  starting transfers between devices  7.33 us (2%)
    psum x2, blocking collectives, norm_part(): sq_power = lax.psum(jnp.sum(hid_f * hid_f, axis=1, keepdims=True), 'x')  32.6 us
    unnamed x6, waiting for transfers between devices  31 us
    all_gather x1, waiting for transfers between devices, local_step(): mlp_slab = lax.all_gather(mlp_cols, 'x', axis=1, tiled=True)  25.4 us
    reduce_scatter x1, waiting for transfers between devices, local_step(): z_cols = lax.psum_scatter(partial_z, 'x', scatter_dimension=1, tiled=True)  25.2 us
    unnamed x13, local copies, waits for them, and re-layouts  25 us
    reduce_scatter x2, waiting for transfers between devices, residual(): lax.psum_scatter(partial_sum.astype(jnp.bfloat16), 'yz', scatter_dimensio...  23.2 us
    all_gather x2, blocking collectives, local_step(): gathered = lax.all_gather(hidden, 'yz', axis=1, tiled=True)  21.7 us
    all_gather x1, blocking collectives, local_step(): attn_slab = lax.all_gather(attn_cols, 'x', axis=1, tiled=True)  16.7 us
  transfers between devices with their start and end apart: 6, of which 6 were waited for; matrix products, arithmetic and copies ran while one was open for 5% of the time, Pallas kernels for 0%

commit v1 on v0

v1 whole, which is shorter than its diff:
```python
import functools

import jax
import jax.numpy as jnp
from jax import lax
from jax.experimental import pallas as pl
from jax.experimental.pallas import tpu as pltpu
from jax.sharding import PartitionSpec as P

NORM_EPS = 1e-5
MESH = pl.DeviceIdType.MESH
F32 = jnp.float32
BF16 = jnp.bfloat16
NT = (((1,), (1,)), ((), ()))
NN = (((1,), (0,)), ((), ()))


def lane_ids(shape):
    return lax.broadcasted_iota(jnp.int32, shape, len(shape) - 1)


def lane_roll(v, shift):
    shift = shift % v.shape[-1]
    return v if shift == 0 else pltpu.roll(v, shift, v.ndim - 1)


def position(ny, nx):
    return lax.axis_index('yz'), lax.axis_index('x')


def peer(y, x, d, ny, nx):
    dy, dx = d // nx, d % nx
    ahead = ((y + dy) % ny, (x + dx) % nx)
    return ahead


def greet_all(y, x, ny, nx):
    barrier = pltpu.get_barrier_semaphore()
    total = ny * nx

    def hello(d, carry):
        py, px = peer(y, x, d, ny, nx)
        pl.semaphore_signal(barrier, inc=1, device_id={'yz': py, 'x': px}, device_id_type=MESH)
        return carry

    lax.fori_loop(1, total, hello, 0)
    return barrier


def remote(src, dst, send_sem, recv_sem, py, px):
    return pltpu.make_async_remote_copy(src_ref=src, dst_ref=dst, send_sem=send_sem, recv_sem=recv_sem,
                                        device_id={'yz': py, 'x': px}, device_id_type=MESH)


def qkv_kernel(ny, nx, cols, rows, width, ht_ref, gain_ref, w_hbm, z_ref, hrow_ref,
               send_buf, recv_buf, w_vmem, gain_col, h_full, u_full, zt_buf, z_send, z_recv, h_rows,
               w_sem, send_sem, recv_sem, zsend_sem, zrecv_sem):
    y, x = position(ny, nx)
    total = ny * nx
    me = x * ny + y
    qcols = w_hbm.shape[0]
    w_copy = pltpu.make_async_copy(w_hbm, w_vmem.at[pl.ds(0, qcols)], w_sem)
    w_copy.start()
    barrier = greet_all(y, x, ny, nx)

    lane = lane_ids((cols, 128))
    lane16 = lane_ids((16, 128))
    tiles = [ht_ref[:, 128 * t:128 * (t + 1)].astype(F32) for t in range(ny)]
    for px in range(nx):
        block = jnp.zeros((cols, 128), F32)
        for t in range(ny):
            piece = lane_roll(tiles[t], rows * t - rows * px)
            block = jnp.where((lane >= rows * t) & (lane < rows * (t + 1)), piece, block)
        high = lane_roll(block[32:48], 64)
        send_buf[px, 0:16] = jnp.where(lane16 < 64, block[0:16], high).astype(BF16)
        send_buf[px, 16:32] = block[16:32].astype(BF16)

    pl.semaphore_wait(barrier, total - 1)

    def send(d, carry):
        py, px = peer(y, x, d, ny, nx)
        remote(send_buf.at[px], recv_buf.at[me], send_sem.at[d], recv_sem.at[d], py, px).start()
        return carry

    lax.fori_loop(1, total, send, 0)
    recv_buf[me] = send_buf[x]

    for j in range(width // 128):
        row = gain_ref[0:1, 128 * j:128 * (j + 1)].astype(F32)
        gain_col[128 * j:128 * (j + 1), :] = jnp.transpose(jnp.broadcast_to(row, (128, 128)))
    w_vmem[qcols:, :] = jnp.zeros((w_vmem.shape[0] - qcols, width), BF16)

    def land(d, carry):
        py, px = peer(y, x, d, ny, nx)
        remote(send_buf.at[px], recv_buf.at[me], send_sem.at[d], recv_sem.at[d], py, px).wait()
        return carry

    lax.fori_loop(1, total, land, 0)

    square = jnp.zeros((16, 128), F32)
    for s in range(total):
        low = recv_buf[s, 0:16].astype(F32)
        mid = recv_buf[s, 16:32].astype(F32)
        high = lane_roll(low, 64)
        h_full[cols * s:cols * s + 16, :] = low
        h_full[cols * s + 16:cols * s + 32, :] = mid
        h_full[cols * s + 32:cols * s + 48, :] = high
        square = square + low * low + mid * mid + high * high
    power = jnp.sum(square, axis=0, keepdims=True)
    inv = lax.rsqrt(power / width + NORM_EPS)
    u_full[...] = (h_full[...] * inv * gain_col[...]).astype(BF16)
    w_copy.wait()
    zt_buf[...] = lax.dot_general(w_vmem[...], u_full[...], NN, preferred_element_type=F32)
    for j in range(zt_buf.shape[0] // 128):
        zj = jnp.transpose(zt_buf[128 * j:128 * (j + 1), :])
        for t in range(ny):
            z_send[t, :, 128 * j:128 * (j + 1)] = zj[rows * t:rows * (t + 1)].astype(BF16)
    for d in range(1, ny):
        py = (y + d) % ny
        remote(z_send.at[py], z_recv.at[y], zsend_sem.at[d], zrecv_sem.at[d], py, x).start()
    z_recv[y] = z_send[y]

    for j in range(width // 128):
        h_rows[:, 128 * j:128 * (j + 1)] = jnp.transpose(h_full[128 * j:128 * (j + 1), :])
    hrow_ref[...] = h_rows[pl.ds(pl.multiple_of(y * rows, rows), rows), :]

    for d in range(1, ny):
        py = (y + d) % ny
        remote(z_send.at[py], z_recv.at[y], zsend_sem.at[d], zrecv_sem.at[d], py, x).wait()

    zs = [[z_recv[t, :, 128 * j:128 * (j + 1)].astype(F32) for j in range(w_vmem.shape[0] // 128)] for t in range(ny)]
    for g in range(ny * qcols // 128):
        start = 128 * g
        t = start // qcols
        off = start - t * qcols
        j, sh = off // 128, off % 128
        take = min(128, qcols - off)
        out = lane_roll(zs[t][j], -sh)
        if sh and take > 128 - sh:
            out = jnp.where(lane16 < 128 - sh, out, lane_roll(zs[t][j + 1], -sh))
        if take < 128:
            out = jnp.where(lane16 < take, out, lane_roll(zs[t + 1][0], take))
        z_ref[:, g, :] = out
    for g in range(ny * qcols // 128, z_ref.shape[1]):
        z_ref[:, g, :] = jnp.zeros((rows, 128), F32)


def attend_kernel(heads, scale, len_ref, z_ref, k_ref, v_ref, o_ref, ko_ref, vo_ref, o_acc):
    b = pl.program_id(0)
    slots = k_ref.shape[1]
    length = len_ref[b]
    base = pl.multiple_of((length // 16) * 16, 16)
    here = lax.broadcasted_iota(jnp.int32, (16, 128), 0) == length - base
    z = z_ref[b]
    ko_ref[...] = k_ref[...]
    vo_ref[...] = v_ref[...]
    k_new = jnp.broadcast_to(z[heads:heads + 1], (16, 128)).astype(BF16)
    v_new = jnp.broadcast_to(z[heads + 1:heads + 2], (16, 128)).astype(BF16)
    ko_ref[0, pl.ds(base, 16), :] = jnp.where(here, k_new, k_ref[0, pl.ds(base, 16), :])
    vo_ref[0, pl.ds(base, 16), :] = jnp.where(here, v_new, v_ref[0, pl.ds(base, 16), :])
    s = lax.dot_general(z.astype(BF16), ko_ref[0], NT, preferred_element_type=F32) * scale
    s = jnp.where(lane_ids(s.shape) <= length, s, -1e30)
    e = jnp.exp(s - jnp.max(s, axis=1, keepdims=True))
    p = (e / jnp.sum(e, axis=1, keepdims=True)).astype(BF16)
    o_acc[b] = lax.dot_general(p, vo_ref[0], NN, preferred_element_type=F32)

    @pl.when(b == pl.num_programs(0) - 1)
    def _():
        for h in range(heads):
            o_ref[h] = o_acc[:, h, :].astype(BF16)


def mlp_kernel(ny, nx, cols, rows, width, heads, o_ref, hrow_ref, gain_ref, wo_hbm, wgu_hbm, wd_hbm, out_ref,
               wo, wgu, wd, o_recv, part, p_send, p_recv, hm_send, hm_recv, hm_cols, tail, u_full, m_cols, m_rows,
               f_part, f_cols, f_send, f_recv,
               wo_sem, wgu_sem, wd_sem, os_sem, or_sem, ps_sem, pr_sem, hs_sem, hr_sem, fs_sem, fr_sem):
    y, x = position(ny, nx)
    total = ny * nx
    me = x * ny + y
    slot = y * nx + x
    heads_y = heads // ny
    many = ny * rows
    ffn = wgu_hbm.shape[1]
    chunk = wgu_sem.shape[0]
    step = ffn // chunk
    wo_copy = pltpu.make_async_copy(wo_hbm, wo, wo_sem)
    wo_copy.start()
    wgu_copies = []
    for c in range(chunk):
        wgu_copies.append(pltpu.make_async_copy(wgu_hbm.at[:, pl.ds(c * step, step)], wgu.at[:, pl.ds(c * step, step)], wgu_sem.at[c]))
        wgu_copies[-1].start()
    wd_copy = pltpu.make_async_copy(wd_hbm, wd.at[pl.ds(0, ffn)], wd_sem)
    wd_copy.start()
    barrier = greet_all(y, x, ny, nx)
    wd[ffn:, :] = jnp.zeros((wd.shape[0] - ffn, width), BF16)
    m_cols[ffn:, :] = jnp.zeros((m_cols.shape[0] - ffn, 128), F32)
    f_part[many:, :] = jnp.zeros((f_part.shape[0] - many, width), F32)
    pl.semaphore_wait(barrier, total - 1)

    def o_copy(d):
        py = (y + d) % ny
        return remote(o_ref.at[pl.ds(py * heads_y, heads_y)], o_recv.at[y], os_sem.at[d], or_sem.at[d], py, x)

    for d in range(1, ny):
        o_copy(d).start()
    o_recv[y] = o_ref[pl.ds(y * heads_y, heads_y)]
    for d in range(1, ny):
        o_copy(d).wait()
    wo_copy.wait()
    o_rows = [jnp.concatenate([o_recv[t, h] for t in range(ny)], axis=0) for h in range(heads_y)]
    o_full = jnp.concatenate(o_rows, axis=1)
    part[...] = lax.dot_general(o_full, wo[...], NN, preferred_element_type=F32)
    for t in range(ny):
        p_send[t] = part[rows * t:rows * (t + 1), :].astype(BF16)

    def p_copy(d):
        py = (y + d) % ny
        return remote(p_send.at[py], p_recv.at[y], ps_sem.at[d], pr_sem.at[d], py, x)

    for d in range(1, ny):
        p_copy(d).start()
    p_recv[y] = p_send[y]
    for d in range(1, ny):
        p_copy(d).wait()
    summed = p_recv[0].astype(F32)
    for t in range(1, ny):
        summed = summed + p_recv[t].astype(F32)
    h_mid = (hrow_ref[...] + summed).astype(BF16)
    hm_send[...] = h_mid

    def h_copy(d):
        py = (y + d) % ny
        return remote(hm_send, hm_recv.at[y], hs_sem.at[d], hr_sem.at[d], py, x)

    for d in range(1, ny):
        h_copy(d).start()
    hm_recv[y] = h_mid

    hm_cols[0:rows, :] = h_mid.astype(F32)
    hm_cols[rows:, :] = jnp.zeros((hm_cols.shape[0] - rows, width), F32)
    for j in range(width // 128):
        f_cols[128 * j:128 * (j + 1), :] = jnp.transpose(hm_cols[:, 128 * j:128 * (j + 1)])
    lane16 = lane_ids((16, 128))
    for s in range(total):
        corner = jnp.zeros((16, 128), F32)
        for k in range(cols // 16):
            corner = corner + lane_roll(f_cols[cols * s + 16 * k:cols * s + 16 * (k + 1), :], 64 + 16 * k)
        tail[s] = corner

    for d in range(1, ny):
        h_copy(d).wait()
    h64 = jnp.concatenate([hm_recv[t] for t in range(ny)], axis=0).astype(F32)
    inv = lax.rsqrt(jnp.sum(h64 * h64, axis=1, keepdims=True) / width + NORM_EPS)
    u_full[...] = (h64 * inv * gain_ref[...].astype(F32)).astype(BF16)

    def gate_up(c, carry):
        at = pl.multiple_of(c * step, step)
        pltpu.make_async_copy(wgu_hbm.at[:, pl.ds(at, step)], wgu.at[:, pl.ds(at, step)], wgu_sem.at[c]).wait()
        gate = lax.dot_general(wgu[0, pl.ds(at, step), :], u_full[...], NT, preferred_element_type=F32)
        up = lax.dot_general(wgu[1, pl.ds(at, step), :], u_full[...], NT, preferred_element_type=F32)
        gate = gate.astype(BF16).astype(F32)
        up = up.astype(BF16).astype(F32)
        m_cols[pl.ds(at, step), 0:many] = jax.nn.silu(gate) * up
        return carry

    m_cols[:, many:] = jnp.zeros((m_cols.shape[0], 128 - many), F32)
    lax.fori_loop(0, chunk, gate_up, 0)
    for j in range(m_rows.shape[1] // 128):
        m_rows[:, 128 * j:128 * (j + 1)] = jnp.transpose(m_cols[128 * j:128 * (j + 1), :])[0:many].astype(BF16)
    wd_copy.wait()
    wide = 256
    for n in range(width // wide):
        f_part[0:many, wide * n:wide * (n + 1)] = lax.dot_general(
            m_rows[...], wd[:, wide * n:wide * (n + 1)], NN, preferred_element_type=F32)
    for j in range(width // 128):
        f_cols[128 * j:128 * (j + 1), :] = jnp.transpose(f_part[:, 128 * j:128 * (j + 1)])
    for s in range(total):
        a0 = f_cols[cols * s:cols * s + 16, :]
        a1 = f_cols[cols * s + 16:cols * s + 32, :]
        a2 = lane_roll(f_cols[cols * s + 32:cols * s + 48, :], 64)
        f_send[s, 0:16] = jnp.where(lane16 < 64, a0, a2).astype(BF16)
        f_send[s, 16:32] = jnp.where(lane16 < 64, a1, tail[s]).astype(BF16)

    def f_copy(d):
        py, px = peer(y, x, d, ny, nx)
        return remote(f_send.at[px * ny + py], f_recv.at[slot], fs_sem.at[d], fr_sem.at[d], py, px)

    def f_start(d, carry):
        f_copy(d).start()
        return carry

    def f_wait(d, carry):
        f_copy(d).wait()
        return carry

    lax.fori_loop(1, total, f_start, 0)
    f_recv[slot] = f_send[me]
    lax.fori_loop(1, total, f_wait, 0)

    sums = [[jnp.zeros((16, 128), F32) for _ in range(3)] for _ in range(ny)]
    olds = [[jnp.zeros((16, 128), F32) for _ in range(3)] for _ in range(ny)]
    for px in range(nx):
        mine = (lane16 >= rows * px) & (lane16 < rows * (px + 1))
        low = f_recv[px, 0:16].astype(F32)
        for t in range(1, ny):
            low = low + f_recv[t * nx + px, 0:16].astype(F32)
        corner = [f_recv[t * nx + px, 16:32].astype(F32) for t in range(ny)]
        mid = corner[0]
        for t in range(1, ny):
            mid = mid + corner[t]
        high = lane_roll(low, 64)
        for t in range(ny):
            for k, v in enumerate((low, mid, high)):
                sums[t][k] = jnp.where(mine, lane_roll(v, rows * px - rows * t), sums[t][k])
                olds[t][k] = jnp.where(mine, lane_roll(corner[t], rows * px - 64 - 16 * k), olds[t][k])
    for t in range(ny):
        for k in range(3):
            out_ref[16 * k:16 * (k + 1), 128 * t:128 * (t + 1)] = (olds[t][k] + sums[t][k]).astype(BF16)


def solution(mesh):
    group_axes = ('yz', 'x')
    batch_axes = ('replica', 'yz', 'x')
    hidden_spec = P('replica', ('x', 'yz'))
    cache_spec = P(None, batch_axes, None, None)
    ny, nx = mesh.shape['yz'], mesh.shape['x']
    vmem = pl.BlockSpec(memory_space=pltpu.VMEM)
    hbm = pl.BlockSpec(memory_space=pl.ANY)
    dma = pltpu.SemaphoreType.DMA

    def layer(ht, seq_lens, attn_gain, mlp_gain, w_qkv, w_out, w_gate_up, w_down, k_cache, v_cache):
        cols = ht.shape[0]
        rows, slots, head_dim = k_cache.shape
        width = attn_gain.shape[1]
        qcols = w_qkv.shape[0]
        qpad = -(-qcols // 128) * 128
        heads = (qcols * ny) // head_dim - 2
        total = ny * nx
        many = ny * rows
        ffn = w_down.shape[0]
        ffn_pad = -(-ffn // 128) * 128
        z, hrow = pl.pallas_call(
            functools.partial(qkv_kernel, ny, nx, cols, rows, width),
            out_shape=(jax.ShapeDtypeStruct((rows, 16, head_dim), F32), jax.ShapeDtypeStruct((rows, width), F32)),
            in_specs=[vmem, vmem, hbm],
            out_specs=(vmem, vmem),
            scratch_shapes=[
                pltpu.VMEM((nx, 32, 128), BF16), pltpu.VMEM((total, 32, 128), BF16), pltpu.VMEM((qpad, width), BF16),
                pltpu.VMEM((width, 128), F32), pltpu.VMEM((width, 128), F32), pltpu.VMEM((width, 128), BF16),
                pltpu.VMEM((qpad, 128), F32), pltpu.VMEM((ny, rows, qpad), BF16), pltpu.VMEM((ny, rows, qpad), BF16),
                pltpu.VMEM((128, width), F32),
                dma, dma((total,)), dma((total,)), dma((ny,)), dma((ny,))],
            compiler_params=pltpu.CompilerParams(collective_id=0, has_side_effects=True, vmem_limit_bytes=24 << 20),
            name='qkv',
        )(ht, attn_gain, w_qkv)
        o, k_new, v_new = pl.pallas_call(
            functools.partial(attend_kernel, heads, head_dim ** -0.5),
            out_shape=(jax.ShapeDtypeStruct((heads, rows, head_dim), BF16),
                       jax.ShapeDtypeStruct(k_cache.shape, BF16), jax.ShapeDtypeStruct(v_cache.shape, BF16)),
            grid_spec=pltpu.PrefetchScalarGridSpec(
                num_scalar_prefetch=1, grid=(rows,),
                in_specs=[pl.BlockSpec((rows, 16, head_dim), lambda b, _: (0, 0, 0)),
                          pl.BlockSpec((1, slots, head_dim), lambda b, _: (b, 0, 0)),
                          pl.BlockSpec((1, slots, head_dim), lambda b, _: (b, 0, 0))],
                out_specs=(pl.BlockSpec((heads, rows, head_dim), lambda b, _: (0, 0, 0)),
                           pl.BlockSpec((1, slots, head_dim), lambda b, _: (b, 0, 0)),
                           pl.BlockSpec((1, slots, head_dim), lambda b, _: (b, 0, 0))),
                scratch_shapes=[pltpu.VMEM((rows, 16, head_dim), F32)]),
            compiler_params=pltpu.CompilerParams(dimension_semantics=('arbitrary',), vmem_limit_bytes=24 << 20),
            name='attend',
        )(seq_lens, z, k_cache, v_cache)
        chunk = 5
        out = pl.pallas_call(
            functools.partial(mlp_kernel, ny, nx, cols, rows, width, heads),
            out_shape=jax.ShapeDtypeStruct(ht.shape, BF16),
            in_specs=[vmem, vmem, vmem, hbm, hbm, hbm],
            out_specs=vmem,
            scratch_shapes=[
                pltpu.VMEM(w_out.shape, BF16), pltpu.VMEM(w_gate_up.shape, BF16), pltpu.VMEM((ffn_pad, width), BF16),
                pltpu.VMEM((ny, heads // ny, rows, head_dim), BF16), pltpu.VMEM((many, width), F32),
                pltpu.VMEM((ny, rows, width), BF16), pltpu.VMEM((ny, rows, width), BF16),
                pltpu.VMEM((rows, width), BF16), pltpu.VMEM((ny, rows, width), BF16),
                pltpu.VMEM((128, width), F32), pltpu.VMEM((total, 16, 128), F32),
                pltpu.VMEM((many, width), BF16), pltpu.VMEM((ffn_pad, 128), F32), pltpu.VMEM((many, ffn_pad), BF16),
                pltpu.VMEM((128, width), F32), pltpu.VMEM((width, 128), F32),
                pltpu.VMEM((total, 32, 128), BF16), pltpu.VMEM((total, 32, 128), BF16),
                dma, dma((chunk,)), dma, dma((ny,)), dma((ny,)), dma((ny,)), dma((ny,)), dma((ny,)), dma((ny,)),
                dma((total,)), dma((total,))],
            compiler_params=pltpu.CompilerParams(collective_id=1, has_side_effects=True, vmem_limit_bytes=44 << 20),
            name='mlp',
        )(o, hrow, mlp_gain, w_out, w_gate_up, w_down)
        return out, k_new, v_new

    def local_step(hidden, seq_lens, attn_gain, mlp_gain, w_qkv, w_out, w_gate_up, w_down, k_cache, v_cache):
        ht = hidden.T
        k_layers = []
        v_layers = []
        for i in range(w_qkv.shape[0]):
            ht, k_new, v_new = layer(ht, seq_lens, attn_gain[i:i + 1], mlp_gain[i:i + 1], w_qkv[i].T, w_out[i],
                                     jnp.transpose(w_gate_up[i], (1, 2, 0)), w_down[i], k_cache[i], v_cache[i])
            k_layers.append(k_new)
            v_layers.append(v_new)
        return ht.T, jnp.stack(k_layers), jnp.stack(v_layers)

    return jax.shard_map(
        local_step,
        mesh=mesh,
        in_specs=(hidden_spec, P(batch_axes), P(None, None), P(None, None), P(None, None, 'yz'), P(None, 'yz', None),
                  P(None, None, None, 'yz'), P(None, 'yz', None), cache_spec, cache_spec),
        out_specs=(hidden_spec, cache_spec, cache_spec),
        check_vma=False)
```

time: 296 us -> 77.2 us (0.26)
  waiting for transfers between devices: 111 us -> 0 us
  blocking collectives: 80.7 us -> 0 us
  Pallas kernels: 0 us -> 65.4 us
  matrix products: 32.9 us -> 0 us
  local copies, waits for them, and re-layouts: 29.9 us -> 10.9 us
  other arithmetic: 17.5 us -> 0 us
  between operations: 14.6 us -> 0.67 us
  starting transfers between devices: 7.33 us -> 0 us
    pallas_call x0 -> x3, Pallas kernels: none -> 65.4 us  [the longest x1 31.2 us: layer(): pl.pallas_call(functools.partial(mlp_kernel, ny, nx, cols, rows, width, h...]
    reduce_scatter x3 -> x0, waiting for transfers between devices: 48.4 us -> none  [the longest x1 25.2 us: local_step(): z_cols = lax.psum_scatter(partial_z, 'x', scatter_dimension=1, tiled=True)]
    all_gather x3 -> x0, blocking collectives: 38.4 us -> none  [the longest x2 21.7 us: local_step(): gathered = lax.all_gather(hidden, 'yz', axis=1, tiled=True)]
    psum x2 -> x0, blocking collectives: 32.6 us -> none  [norm_part(): sq_power = lax.psum(jnp.sum(hid_f * hid_f, axis=1, keepdims=True), 'x')]
    unnamed x6 -> x0, waiting for transfers between devices: 31 us -> none
    all_gather x1 -> x0, waiting for transfers between devices: 25.4 us -> none  [local_step(): mlp_slab = lax.all_gather(mlp_cols, 'x', axis=1, tiled=True)]
    dot_general x5 -> x0, matrix products: 22.5 us -> none  [the longest x1 9.22 us: attend(): jnp.einsum('bhs,bsd->bhd', probs_bf, v_upd, preferred_element_type=jnp.fl...]
    unnamed x13 -> x19, local copies, waits for them, and re-layouts: 25 us -> 10.9 us
  transfers between devices with their start and end apart: 6 -> 0, of which waited for: 6 -> 0; matrix products, arithmetic and copies ran while one was open for 5% -> 0% of each run, Pallas kernels for 0% -> 0%
where the time goes in v1:
time: 77.2 us; the launch traced here: 76.9 us
  Pallas kernels  65.4 us (85%)
  local copies, waits for them, and re-layouts  10.9 us (14%)
    pallas_call x1, Pallas kernels, layer(): pl.pallas_call(functools.partial(mlp_kernel, ny, nx, cols, rows, width, h...  31.2 us
    pallas_call x1, Pallas kernels, layer(): pl.pallas_call(functools.partial(qkv_kernel, ny, nx, cols, rows, width),...  20 us
    pallas_call x1, Pallas kernels, layer(): pl.pallas_call(functools.partial(attend_kernel, heads, head_dim ** (-0.5)...  14.2 us
    unnamed x19, local copies, waits for them, and re-layouts  10.9 us

profile of v1, /device:TPU:97, one launch (start us, length us, event | category | flops | bytes accessed | tf_op | source)
XLA Modules:
  0.0 76.9 jit_solution(14957621006810572168)
XLA Ops:
  0.6 0.0 copy-start.3
  0.6 1.3 %copy-done.3 = bf16[1,1536,448]{1,2,0:T(8,128)(2,1)S(1)} copy-done((bf16[1,1536,448]{1,2,0:T(8,128)(2,1)S(1)}, bf16[1,1536,448]{1,2,0:T(8,128)(2,1)}, u32[]{:S(2)}) %copy-start.3) | copy-done | bytes 1376280
  2.0 0.0 copy-start.5
  2.0 0.8 %copy-done.5 = bf16[512,48]{0,1:T(8,128)(2,1)S(1)} copy-done((bf16[512,48]{0,1:T(8,128)(2,1)S(1)}, bf16[512,48]{0,1:T(8,128)(2,1)}, u32[]{:S(2)}) %copy-start.5) | copy-done | bytes 49176
  2.8 0.0 copy-start.7
  2.8 0.7 copy-done.7
  3.5 20.0 %qkv.1 = (f32[16,16,128]{2,1,0:T(8,128)S(1)}, f32[16,1536]{1,0:T(8,128)S(1)}) custom-call(bf16[48,512]{1,0:T(8,128)(2,1)S(1)} %bitcast.20, bf16[1,1536]{1,0:T(2,128)(2,1)S(1)} %copy-done.7, bf16[448,1536]{1,0:T(8,128)(2,1)S(1)} %bitcast.17), custom_call_target="tpu_custom_call" | custom-call | tf_op jit(solution)/shard_map/qkv/pallas_call | solution.py:342
  23.5 0.0 copy-start
  23.5 3.4 %copy-done = bf16[1,16,2048,128]{3,2,1,0:T(8,128)(2,1)S(1)} copy-done((bf16[1,16,2048,128]{3,2,1,0:T(8,128)(2,1)S(1)}, bf16[1,16,2048,128]{3,2,1,0:T(8,128)(2,1)}, u32[]{:S(2)}) %copy-start) | copy-done | bytes 8388632
  26.9 0.0 copy-start.1
  26.9 3.4 %copy-done.1 = bf16[1,16,2048,128]{3,2,1,0:T(8,128)(2,1)S(1)} copy-done((bf16[1,16,2048,128]{3,2,1,0:T(8,128)(2,1)S(1)}, bf16[1,16,2048,128]{3,2,1,0:T(8,128)(2,1)}, u32[]{:S(2)}) %copy-start.1) | copy-done | bytes 8388632
  30.2 0.0 copy-start.8
  30.3 0.7 copy-done.8
  30.9 0.0 copy-start.2
  30.9 0.0 copy-start.4
  30.9 0.0 copy-start.6
  30.9 14.2 %attend.1 = (bf16[12,16,128]{2,1,0:T(8,128)(2,1)S(1)}, bf16[16,2048,128]{2,1,0:T(8,128)(2,1)}, bf16[16,2048,128]{2,1,0:T(8,128)(2,1)}) custom-call(s32[16]{0:T(128)S(1)} %copy-done.8, f32[16,16,128]{2,1,0:T(8,128)S(1)} %get-tuple-element.8.z_ref, bf16[16,2048,128]{2,1,0:T(8,128)(2,1)S(1)} %bitcast.14, bf16[16,2048,128]{2,1,0:T(8,128)(2,1)S(1)} %bitcast.15), custom_call_target="tpu_custom_call" | custom-call | tf_op jit(solution)/shard_map/attend/pallas_call | solution.py:356
  45.1 0.0 copy-done.2
  45.1 0.0 copy-done.4
  45.1 0.0 copy-done.6
  45.1 31.2 %mlp.1 = bf16[48,512]{1,0:T(8,128)(2,1)S(1)} custom-call(bf16[12,16,128]{2,1,0:T(8,128)(2,1)S(1)} %get-tuple-element.9.o_ref, f32[16,1536]{1,0:T(8,128)S(1)} %get-tuple-element.10.hrow_ref, bf16[1,1536]{1,0:T(2,128)(2,1)S(1)} %copy-done.6, bf16[384,1536]{1,0:T(8,128)(2,1)S(1)} %bitcast.18, bf16[2,2240,1536]{2,1,0:T(8,128)(2,1)} %bitcast.21, ...), custom_call_target="tpu_custom_call" | custom-call | tf_op jit(solution)/shard_map/mlp/pallas_call | solution.py:373
  76.3 0.6 copy.14
Async XLA Ops:
  0.6 1.3 %copy-start.3 = (bf16[1,1536,448]{1,2,0:T(8,128)(2,1)S(1)}, bf16[1,1536,448]{1,2,0:T(8,128)(2,1)}, u32[]{:S(2)}) copy-start(bf16[1,1536,448]{1,2,0:T(8,128)(2,1)} %param.14) | copy-start | bytes 4128772
  2.0 0.8 %copy-start.5 = (bf16[512,48]{0,1:T(8,128)(2,1)S(1)}, bf16[512,48]{0,1:T(8,128)(2,1)}, u32[]{:S(2)}) copy-start(bf16[512,48]{0,1:T(8,128)(2,1)} %param.10) | copy-start | bytes 147460
  2.8 0.7 copy-start.7
  23.5 3.4 %copy-start = (bf16[1,16,2048,128]{3,2,1,0:T(8,128)(2,1)S(1)}, bf16[1,16,2048,128]{3,2,1,0:T(8,128)(2,1)}, u32[]{:S(2)}) copy-start(bf16[1,16,2048,128]{3,2,1,0:T(8,128)(2,1)} %param.18) | copy-start | bytes 25165828
  26.9 3.4 %copy-start.1 = (bf16[1,16,2048,128]{3,2,1,0:T(8,128)(2,1)S(1)}, bf16[1,16,2048,128]{3,2,1,0:T(8,128)(2,1)}, u32[]{:S(2)}) copy-start(bf16[1,16,2048,128]{3,2,1,0:T(8,128)(2,1)} %param.19) | copy-start | bytes 25165828
  30.2 0.7 copy-start.8
  30.9 14.2 %copy-start.2 = (bf16[1,2240,1536]{2,1,0:T(8,128)(2,1)S(1)}, bf16[1,2240,1536]{2,1,0:T(8,128)(2,1)}, u32[]{:S(2)}) copy-start(bf16[1,2240,1536]{2,1,0:T(8,128)(2,1)} %param.17) | copy-start | bytes 20643844
  30.9 14.2 %copy-start.4 = (bf16[1,384,1536]{2,1,0:T(8,128)(2,1)S(1)}, bf16[1,384,1536]{2,1,0:T(8,128)(2,1)}, u32[]{:S(2)}) copy-start(bf16[1,384,1536]{2,1,0:T(8,128)(2,1)} %param.15) | copy-start | bytes 3538948
  30.9 14.2 %copy-start.6 = (bf16[1,1536]{1,0:T(2,128)(2,1)S(1)}, bf16[1,1536]{1,0:T(2,128)(2,1)}, u32[]{:S(2)}) copy-start(bf16[1,1536]{1,0:T(2,128)(2,1)} %gain_ref.3) | copy-start | bytes 9220

commit v2 on v1

--- a/solution.py
+++ b/solution.py
@@ -52,16 +52,27 @@
                                         device_id={'yz': py, 'x': px}, device_id_type=MESH)
 
 
-def qkv_kernel(ny, nx, cols, rows, width, ht_ref, gain_ref, w_hbm, z_ref, hrow_ref,
-               send_buf, recv_buf, w_vmem, gain_col, h_full, u_full, zt_buf, z_send, z_recv, h_rows,
-               w_sem, send_sem, recv_sem, zsend_sem, zrecv_sem):
+def qkv_kernel(ny, nx, cols, rows, width, ht_hbm, gain_hbm, w_hbm, k_hbm, v_hbm, z_ref, hrow_ref, k_ref, v_ref,
+               ht_ref, gain_ref, send_buf, recv_buf, w_vmem, gain_col, h_full, u_full, zt_buf, z_send, z_recv, h_rows,
+               h_sem, g_sem, w_sem, kv_sem, send_sem, recv_sem, zsend_sem, zrecv_sem):
     y, x = position(ny, nx)
     total = ny * nx
     me = x * ny + y
     qcols = w_hbm.shape[0]
+    h_copy = pltpu.make_async_copy(ht_hbm, ht_ref, h_sem)
+    h_copy.start()
+    barrier = greet_all(y, x, ny, nx)
+    g_copy = pltpu.make_async_copy(gain_hbm, gain_ref, g_sem)
+    g_copy.start()
     w_copy = pltpu.make_async_copy(w_hbm, w_vmem.at[pl.ds(0, qcols)], w_sem)
     w_copy.start()
-    barrier = greet_all(y, x, ny, nx)
+    parts = kv_sem.shape[1]
+    share = k_hbm.shape[0] // parts
+    kv_copies = [pltpu.make_async_copy(src.at[pl.ds(i * share, share)], dst.at[pl.ds(i * share, share)], kv_sem.at[c, i])
+                 for i in range(parts) for c, (src, dst) in enumerate(((k_hbm, k_ref), (v_hbm, v_ref)))]
+    for copy in kv_copies:
+        copy.start()
+    h_copy.wait()
 
     lane = lane_ids((cols, 128))
     lane16 = lane_ids((16, 128))
@@ -85,6 +96,7 @@
     lax.fori_loop(1, total, send, 0)
     recv_buf[me] = send_buf[x]
 
+    g_copy.wait()
     for j in range(width // 128):
         row = gain_ref[0:1, 128 * j:128 * (j + 1)].astype(F32)
         gain_col[128 * j:128 * (j + 1), :] = jnp.transpose(jnp.broadcast_to(row, (128, 128)))
@@ -143,37 +155,71 @@
         z_ref[:, g, :] = out
     for g in range(ny * qcols // 128, z_ref.shape[1]):
         z_ref[:, g, :] = jnp.zeros((rows, 128), F32)
-
-
-def attend_kernel(heads, scale, len_ref, z_ref, k_ref, v_ref, o_ref, ko_ref, vo_ref, o_acc):
-    b = pl.program_id(0)
-    slots = k_ref.shape[1]
-    length = len_ref[b]
-    base = pl.multiple_of((length // 16) * 16, 16)
-    here = lax.broadcasted_iota(jnp.int32, (16, 128), 0) == length - base
-    z = z_ref[b]
-    ko_ref[...] = k_ref[...]
-    vo_ref[...] = v_ref[...]
-    k_new = jnp.broadcast_to(z[heads:heads + 1], (16, 128)).astype(BF16)
-    v_new = jnp.broadcast_to(z[heads + 1:heads + 2], (16, 128)).astype(BF16)
-    ko_ref[0, pl.ds(base, 16), :] = jnp.where(here, k_new, k_ref[0, pl.ds(base, 16), :])
-    vo_ref[0, pl.ds(base, 16), :] = jnp.where(here, v_new, v_ref[0, pl.ds(base, 16), :])
-    s = lax.dot_general(z.astype(BF16), ko_ref[0], NT, preferred_element_type=F32) * scale
-    s = jnp.where(lane_ids(s.shape) <= length, s, -1e30)
-    e = jnp.exp(s - jnp.max(s, axis=1, keepdims=True))
-    p = (e / jnp.sum(e, axis=1, keepdims=True)).astype(BF16)
-    o_acc[b] = lax.dot_general(p, vo_ref[0], NN, preferred_element_type=F32)
-
-    @pl.when(b == pl.num_programs(0) - 1)
-    def _():
-        for h in range(heads):
-            o_ref[h] = o_acc[:, h, :].astype(BF16)
-
-
-def mlp_kernel(ny, nx, cols, rows, width, heads, o_ref, hrow_ref, gain_ref, wo_hbm, wgu_hbm, wd_hbm, out_ref,
-               wo, wgu, wd, o_recv, part, p_send, p_recv, hm_send, hm_recv, hm_cols, tail, u_full, m_cols, m_rows,
+    for copy in kv_copies:
+        copy.wait()
+
+
+def attend_kernel(heads, scale, len_ref, z_ref, k_in, v_in, k_hbm, v_hbm, o_ref, k_ref, v_ref, s_buf, o_acc, k_sem, v_sem):
+    rows, slots = k_ref.shape[:2]
+
+    def place(b, carry):
+        length = len_ref[b]
+        base = pl.multiple_of((length // 16) * 16, 16)
+        here = lax.broadcasted_iota(jnp.int32, (16, 128), 0) == length - base
+        k_new = jnp.broadcast_to(z_ref[b, heads:heads + 1, :], (16, 128)).astype(BF16)
+        v_new = jnp.broadcast_to(z_ref[b, heads + 1:heads + 2, :], (16, 128)).astype(BF16)
+        k_ref[b, pl.ds(base, 16), :] = jnp.where(here, k_new, k_ref[b, pl.ds(base, 16), :])
+        v_ref[b, pl.ds(base, 16), :] = jnp.where(here, v_new, v_ref[b, pl.ds(base, 16), :])
+        return carry
+
+    def k_copy(b):
+        return pltpu.make_async_copy(k_ref.at[b], k_hbm.at[b], k_sem.at[b])
+
+    def v_copy(b):
+        return pltpu.make_async_copy(v_ref.at[b], v_hbm.at[b], v_sem.at[b])
+
+    def leave(b, carry):
+        k_copy(b).start()
+        v_copy(b).start()
+        return carry
+
+    def score(b):
+        s = lax.dot_general(z_ref[b].astype(BF16), k_ref[b], NT, preferred_element_type=F32) * scale
+        s_buf[b % 2] = s
+
+    def finish(b):
+        s = s_buf[b % 2]
+        s = jnp.where(lane_ids(s.shape) <= len_ref[b], s, -1e30)
+        e = jnp.exp(s - jnp.max(s, axis=1, keepdims=True))
+        p = (e * (1.0 / jnp.sum(e, axis=1, keepdims=True))).astype(BF16)
+        o_acc[b] = lax.dot_general(p, v_ref[b], NN, preferred_element_type=F32)
+
+    lax.fori_loop(0, rows, place, 0)
+    lax.fori_loop(0, rows, leave, 0)
+    score(0)
+
+    def step(b, carry):
+        score(b + 1)
+        finish(b)
+        return carry
+
+    lax.fori_loop(0, rows - 1, step, 0)
+    finish(rows - 1)
+    for h in range(heads):
+        o_ref[h] = o_acc[:, h, :].astype(BF16)
+
+    def drain(b, carry):
+        k_copy(b).wait()
+        v_copy(b).wait()
+        return carry
+
+    lax.fori_loop(0, rows, drain, 0)
+
+
+def mlp_kernel(ny, nx, cols, rows, width, heads, o_ref, hrow_ref, gain_hbm, wo_hbm, wgu_hbm, wd_hbm, out_ref,
+               gain_ref, wo, wgu, wd, o_recv, part, p_send, p_recv, hm_send, hm_recv, hm_cols, tail, u_full, m_cols, m_rows,
                f_part, f_cols, f_send, f_recv,
-               wo_sem, wgu_sem, wd_sem, os_sem, or_sem, ps_sem, pr_sem, hs_sem, hr_sem, fs_sem, fr_sem):
+               gain_sem, wo_sem, wgu_sem, wd_sem, os_sem, or_sem, ps_sem, pr_sem, hs_sem, hr_sem, fs_sem, fr_sem):
     y, x = position(ny, nx)
     total = ny * nx
     me = x * ny + y
@@ -183,6 +229,8 @@
     ffn = wgu_hbm.shape[1]
     chunk = wgu_sem.shape[0]
     step = ffn // chunk
+    gain_copy = pltpu.make_async_copy(gain_hbm, gain_ref, gain_sem)
+    gain_copy.start()
     wo_copy = pltpu.make_async_copy(wo_hbm, wo, wo_sem)
     wo_copy.start()
     wgu_copies = []
@@ -249,6 +297,7 @@
 
     for d in range(1, ny):
         h_copy(d).wait()
+    gain_copy.wait()
     h64 = jnp.concatenate([hm_recv[t] for t in range(ny)], axis=0).astype(F32)
     inv = lax.rsqrt(jnp.sum(h64 * h64, axis=1, keepdims=True) / width + NORM_EPS)
     u_full[...] = (h64 * inv * gain_ref[...].astype(F32)).astype(BF16)
@@ -339,43 +388,46 @@
         many = ny * rows
         ffn = w_down.shape[0]
         ffn_pad = -(-ffn // 128) * 128
-        z, hrow = pl.pallas_call(
+        in_hbm = functools.partial(pltpu.with_memory_space_constraint, memory_space=pltpu.HBM)
+        parts = 4
+        z, hrow, k_vmem, v_vmem = pl.pallas_call(
             functools.partial(qkv_kernel, ny, nx, cols, rows, width),
-            out_shape=(jax.ShapeDtypeStruct((rows, 16, head_dim), F32), jax.ShapeDtypeStruct((rows, width), F32)),
-            in_specs=[vmem, vmem, hbm],
-            out_specs=(vmem, vmem),
+            out_shape=(jax.ShapeDtypeStruct((rows, 16, head_dim), F32), jax.ShapeDtypeStruct((rows, width), F32),
+                       pltpu.VMEM(k_cache.shape, BF16), pltpu.VMEM(v_cache.shape, BF16)),
+            in_specs=[hbm] * 5,
+            out_specs=(vmem,) * 4,
             scratch_shapes=[
+                pltpu.VMEM(ht.shape, BF16), pltpu.VMEM(attn_gain.shape, BF16),
                 pltpu.VMEM((nx, 32, 128), BF16), pltpu.VMEM((total, 32, 128), BF16), pltpu.VMEM((qpad, width), BF16),
                 pltpu.VMEM((width, 128), F32), pltpu.VMEM((width, 128), F32), pltpu.VMEM((width, 128), BF16),
                 pltpu.VMEM((qpad, 128), F32), pltpu.VMEM((ny, rows, qpad), BF16), pltpu.VMEM((ny, rows, qpad), BF16),
                 pltpu.VMEM((128, width), F32),
-                dma, dma((total,)), dma((total,)), dma((ny,)), dma((ny,))],
-            compiler_params=pltpu.CompilerParams(collective_id=0, has_side_effects=True, vmem_limit_bytes=24 << 20),
+                dma, dma, dma, dma((2, parts)), dma((total,)), dma((total,)), dma((ny,)), dma((ny,))],
+            compiler_params=pltpu.CompilerParams(collective_id=0, has_side_effects=True, vmem_limit_bytes=12 << 20),
+            cost_estimate=pl.CostEstimate(flops=8_000_000_000, bytes_accessed=20_000_000, transcendentals=0),
             name='qkv',
-        )(ht, attn_gain, w_qkv)
-        o, k_new, v_new = pl.pallas_call(
+        )(in_hbm(ht), in_hbm(attn_gain), in_hbm(w_qkv), in_hbm(k_cache), in_hbm(v_cache))
+        k_new, v_new, o, _, _ = pl.pallas_call(
             functools.partial(attend_kernel, heads, head_dim ** -0.5),
-            out_shape=(jax.ShapeDtypeStruct((heads, rows, head_dim), BF16),
-                       jax.ShapeDtypeStruct(k_cache.shape, BF16), jax.ShapeDtypeStruct(v_cache.shape, BF16)),
-            grid_spec=pltpu.PrefetchScalarGridSpec(
-                num_scalar_prefetch=1, grid=(rows,),
-                in_specs=[pl.BlockSpec((rows, 16, head_dim), lambda b, _: (0, 0, 0)),
-                          pl.BlockSpec((1, slots, head_dim), lambda b, _: (b, 0, 0)),
-                          pl.BlockSpec((1, slots, head_dim), lambda b, _: (b, 0, 0))],
-                out_specs=(pl.BlockSpec((heads, rows, head_dim), lambda b, _: (0, 0, 0)),
-                           pl.BlockSpec((1, slots, head_dim), lambda b, _: (b, 0, 0)),
-                           pl.BlockSpec((1, slots, head_dim), lambda b, _: (b, 0, 0))),
-                scratch_shapes=[pltpu.VMEM((rows, 16, head_dim), F32)]),
-            compiler_params=pltpu.CompilerParams(dimension_semantics=('arbitrary',), vmem_limit_bytes=24 << 20),
+            out_shape=(pltpu.HBM(k_cache.shape, BF16), pltpu.HBM(v_cache.shape, BF16),
+                       jax.ShapeDtypeStruct((heads, rows, head_dim), BF16),
+                       pltpu.VMEM(k_cache.shape, BF16), pltpu.VMEM(v_cache.shape, BF16)),
+            in_specs=[pl.BlockSpec(memory_space=pltpu.SMEM), vmem, vmem, vmem],
+            out_specs=(hbm, hbm, vmem, vmem, vmem),
+            input_output_aliases={2: 3, 3: 4},
+            scratch_shapes=[pltpu.VMEM((2, 16, slots), F32), pltpu.VMEM((rows, 16, head_dim), F32), dma((rows,)), dma((rows,))],
+            compiler_params=pltpu.CompilerParams(vmem_limit_bytes=8 << 20),
+            cost_estimate=pl.CostEstimate(flops=8_000_000_000, bytes_accessed=20_000_000, transcendentals=0),
             name='attend',
-        )(seq_lens, z, k_cache, v_cache)
+        )(seq_lens, z, k_vmem, v_vmem)
         chunk = 5
         out = pl.pallas_call(
             functools.partial(mlp_kernel, ny, nx, cols, rows, width, heads),
             out_shape=jax.ShapeDtypeStruct(ht.shape, BF16),
-            in_specs=[vmem, vmem, vmem, hbm, hbm, hbm],
+            in_specs=[vmem, vmem, hbm, hbm, hbm, hbm],
             out_specs=vmem,
             scratch_shapes=[
+                pltpu.VMEM(mlp_gain.shape, BF16),
                 pltpu.VMEM(w_out.shape, BF16), pltpu.VMEM(w_gate_up.shape, BF16), pltpu.VMEM((ffn_pad, width), BF16),
                 pltpu.VMEM((ny, heads // ny, rows, head_dim), BF16), pltpu.VMEM((many, width), F32),
                 pltpu.VMEM((ny, rows, width), BF16), pltpu.VMEM((ny, rows, width), BF16),
@@ -384,11 +436,11 @@
                 pltpu.VMEM((many, width), BF16), pltpu.VMEM((ffn_pad, 128), F32), pltpu.VMEM((many, ffn_pad), BF16),
                 pltpu.VMEM((128, width), F32), pltpu.VMEM((width, 128), F32),
                 pltpu.VMEM((total, 32, 128), BF16), pltpu.VMEM((total, 32, 128), BF16),
-                dma, dma((chunk,)), dma, dma((ny,)), dma((ny,)), dma((ny,)), dma((ny,)), dma((ny,)), dma((ny,)),
+                dma, dma, dma((chunk,)), dma, dma((ny,)), dma((ny,)), dma((ny,)), dma((ny,)), dma((ny,)), dma((ny,)),
                 dma((total,)), dma((total,))],
             compiler_params=pltpu.CompilerParams(collective_id=1, has_side_effects=True, vmem_limit_bytes=44 << 20),
             name='mlp',
-        )(o, hrow, mlp_gain, w_out, w_gate_up, w_down)
+        )(o, hrow, in_hbm(mlp_gain), in_hbm(w_out), in_hbm(w_gate_up), in_hbm(w_down))
         return out, k_new, v_new
 
     def local_step(hidden, seq_lens, attn_gain, mlp_gain, w_qkv, w_out, w_gate_up, w_down, k_cache, v_cache):

time: 77.2 us -> 63 us (0.82)
  local copies, waits for them, and re-layouts: 10.9 us -> 0.63 us
  Pallas kernels: 65.4 us -> 61.6 us
    unnamed x19 -> x3, local copies, waits for them, and re-layouts: 10.9 us -> 0.63 us
    pallas_call x1, Pallas kernels: 14.2 us -> 11.3 us  [layer(): pl.pallas_call(functools.partial(attend_kernel, heads, head_dim ** (-0.5)...]
    pallas_call x1, Pallas kernels: 31.2 us -> 30.4 us  [layer(): pl.pallas_call(functools.partial(mlp_kernel, ny, nx, cols, rows, width, h...]
where the time goes in v2:
time: 63 us; the launch traced here: 62.9 us
  Pallas kernels  61.6 us (98%)
  between operations  0.67 us (1%)
  local copies, waits for them, and re-layouts  0.63 us (1%)
    pallas_call x1, Pallas kernels, layer(): pl.pallas_call(functools.partial(mlp_kernel, ny, nx, cols, rows, width, h...  30.4 us
    pallas_call x1, Pallas kernels, layer(): pl.pallas_call(functools.partial(qkv_kernel, ny, nx, cols, rows, width),...  20 us
    pallas_call x1, Pallas kernels, layer(): pl.pallas_call(functools.partial(attend_kernel, heads, head_dim ** (-0.5)...  11.3 us

profile of v2, /device:TPU:97, one launch (start us, length us, event | category | flops | bytes accessed | tf_op | source)
XLA Modules:
  0.0 62.9 jit_solution(992244999489146836)
XLA Ops:
  0.6 0.0 copy-start
  0.6 20.0 %qkv.1 = (f32[16,16,128]{2,1,0:T(8,128)S(1)}, f32[16,1536]{1,0:T(8,128)S(1)}, bf16[16,2048,128]{2,1,0:T(8,128)(2,1)S(1)}, bf16[16,2048,128]{2,1,0:T(8,128)(2,1)S(1)}) custom-call(bf16[48,512]{1,0:T(8,128)(2,1)} %bitcast.21, bf16[1,1536]{1,0:T(2,128)(2,1)} %gain_hbm.2, bf16[448,1536]{1,0:T(8,128)(2,1)} %bitcast.20, bf16[16,2048,128]{2,1,0:T(8,128)(2,1)} %bitcast.18, ...), custom_call_target="tpu_custom_call" | custom-call | flops 8000000000 | bytes 20000000 | tf_op jit(solution)/shard_map/qkv/pallas_call | solution.py:393
  20.6 0.0 copy-done
  20.6 11.3 %attend.1 = (bf16[16,2048,128]{2,1,0:T(8,128)(2,1)}, bf16[16,2048,128]{2,1,0:T(8,128)(2,1)}, bf16[12,16,128]{2,1,0:T(8,128)(2,1)S(1)}, bf16[16,2048,128]{2,1,0:T(8,128)(2,1)S(1)}, bf16[16,2048,128]{2,1,0:T(8,128)(2,1)S(1)}) custom-call(s32[16]{0:T(128)S(1)} %copy-done, ...), custom_call_target="tpu_custom_call", output_to_operand_aliasing={{3}: (2, {}), {4}: (3, {})} | custom-call | flops 8000000000 | bytes 20000000 | tf_op jit(solution)/shard_map/attend/pallas_call | solution.py:410
  32.0 30.4 %mlp.1 = bf16[48,512]{1,0:T(8,128)(2,1)S(1)} custom-call(bf16[12,16,128]{2,1,0:T(8,128)(2,1)S(1)} %get-tuple-element.13.o_ref, f32[16,1536]{1,0:T(8,128)S(1)} %get-tuple-element.14.hrow_ref, bf16[1,1536]{1,0:T(2,128)(2,1)} %gain_hbm.3, bf16[384,1536]{1,0:T(8,128)(2,1)} %bitcast.17, bf16[2,2240,1536]{2,1,0:T(8,128)(2,1)} %bitcast.15, bf16[2240,1536]{1,0:T(8,128)(2,1)} %bitcast.16), custom_call_target="tpu_custom_call" | custom-call | tf_op jit(solution)/shard_map/mlp/pallas_call | solution.py:424
  62.3 0.6 copy.18
Async XLA Ops:
  0.6 20.0 %copy-start = (s32[16]{0:T(128)S(1)}, s32[16]{0:T(128)}, u32[]{:S(2)}) copy-start(s32[16]{0:T(128)} %len_ref.1) | copy-start | bytes 196

commit v3 on v2

--- a/solution.py
+++ b/solution.py
@@ -28,22 +28,18 @@
     return lax.axis_index('yz'), lax.axis_index('x')
 
 
-def peer(y, x, d, ny, nx):
-    dy, dx = d // nx, d % nx
-    ahead = ((y + dy) % ny, (x + dx) % nx)
-    return ahead
-
-
-def greet_all(y, x, ny, nx):
+def peers(y, x, ny, nx):
+    ys = [(y + d) % ny for d in range(ny)]
+    xs = [(x + d) % nx for d in range(nx)]
+    far_y = sorted(range(ny), key=lambda d: -min(d, ny - d))
+    far_x = sorted(range(nx), key=lambda d: -min(d, nx - d))
+    return [(dy * nx + dx, ys[dy], xs[dx]) for dx in far_x for dy in far_y if dy or dx]
+
+
+def greet_all(others):
     barrier = pltpu.get_barrier_semaphore()
-    total = ny * nx
-
-    def hello(d, carry):
-        py, px = peer(y, x, d, ny, nx)
+    for _, py, px in others:
         pl.semaphore_signal(barrier, inc=1, device_id={'yz': py, 'x': px}, device_id_type=MESH)
-        return carry
-
-    lax.fori_loop(1, total, hello, 0)
     return barrier
 
 
@@ -61,7 +57,8 @@
     qcols = w_hbm.shape[0]
     h_copy = pltpu.make_async_copy(ht_hbm, ht_ref, h_sem)
     h_copy.start()
-    barrier = greet_all(y, x, ny, nx)
+    others = peers(y, x, ny, nx)
+    barrier = greet_all(others)
     g_copy = pltpu.make_async_copy(gain_hbm, gain_ref, g_sem)
     g_copy.start()
     w_copy = pltpu.make_async_copy(w_hbm, w_vmem.at[pl.ds(0, qcols)], w_sem)
@@ -88,12 +85,9 @@
 
     pl.semaphore_wait(barrier, total - 1)
 
-    def send(d, carry):
-        py, px = peer(y, x, d, ny, nx)
-        remote(send_buf.at[px], recv_buf.at[me], send_sem.at[d], recv_sem.at[d], py, px).start()
-        return carry
-
-    lax.fori_loop(1, total, send, 0)
+    h_sends = [remote(send_buf.at[px], recv_buf.at[me], send_sem.at[d], recv_sem.at[d], py, px) for d, py, px in others]
+    for copy in h_sends:
+        copy.start()
     recv_buf[me] = send_buf[x]
 
     g_copy.wait()
@@ -102,12 +96,8 @@
         gain_col[128 * j:128 * (j + 1), :] = jnp.transpose(jnp.broadcast_to(row, (128, 128)))
     w_vmem[qcols:, :] = jnp.zeros((w_vmem.shape[0] - qcols, width), BF16)
 
-    def land(d, carry):
-        py, px = peer(y, x, d, ny, nx)
-        remote(send_buf.at[px], recv_buf.at[me], send_sem.at[d], recv_sem.at[d], py, px).wait()
-        return carry
-
-    lax.fori_loop(1, total, land, 0)
+    for copy in h_sends:
+        copy.wait()
 
     square = jnp.zeros((16, 128), F32)
     for s in range(total):
@@ -183,28 +173,36 @@
         v_copy(b).start()
         return carry
 
-    def score(b):
-        s = lax.dot_general(z_ref[b].astype(BF16), k_ref[b], NT, preferred_element_type=F32) * scale
-        s_buf[b % 2] = s
-
-    def finish(b):
-        s = s_buf[b % 2]
-        s = jnp.where(lane_ids(s.shape) <= len_ref[b], s, -1e30)
+    def score(i):
+        blank = jnp.zeros((16, 128), BF16)
+        q0, q1 = z_ref[2 * i].astype(BF16), z_ref[2 * i + 1].astype(BF16)
+        q = jnp.concatenate([jnp.concatenate([q0, blank], axis=1), jnp.concatenate([blank, q1], axis=1)], axis=0)
+        keys = jnp.concatenate([k_ref[2 * i], k_ref[2 * i + 1]], axis=1)
+        s_buf[i % 2] = lax.dot_general(q, keys, NT, preferred_element_type=F32) * scale
+
+    def finish(i):
+        s = s_buf[i % 2]
+        first = lax.broadcasted_iota(jnp.int32, (32, 1), 0) < 16
+        length = jnp.where(first, len_ref[2 * i], len_ref[2 * i + 1])
+        s = jnp.where(lane_ids(s.shape) <= length, s, -1e30)
         e = jnp.exp(s - jnp.max(s, axis=1, keepdims=True))
         p = (e * (1.0 / jnp.sum(e, axis=1, keepdims=True))).astype(BF16)
-        o_acc[b] = lax.dot_general(p, v_ref[b], NN, preferred_element_type=F32)
+        values = jnp.concatenate([v_ref[2 * i], v_ref[2 * i + 1]], axis=1)
+        o = lax.dot_general(p, values, NN, preferred_element_type=F32)
+        o_acc[2 * i] = o[0:16, 0:128]
+        o_acc[2 * i + 1] = o[16:32, 128:256]
 
     lax.fori_loop(0, rows, place, 0)
     lax.fori_loop(0, rows, leave, 0)
     score(0)
 
-    def step(b, carry):
-        score(b + 1)
-        finish(b)
+    def step(i, carry):
+        score(i + 1)
+        finish(i)
         return carry
 
-    lax.fori_loop(0, rows - 1, step, 0)
-    finish(rows - 1)
+    lax.fori_loop(0, rows // 2 - 1, step, 0)
+    finish(rows // 2 - 1)
     for h in range(heads):
         o_ref[h] = o_acc[:, h, :].astype(BF16)
 
@@ -217,7 +215,7 @@
 
 
 def mlp_kernel(ny, nx, cols, rows, width, heads, o_ref, hrow_ref, gain_hbm, wo_hbm, wgu_hbm, wd_hbm, out_ref,
-               gain_ref, wo, wgu, wd, o_recv, part, p_send, p_recv, hm_send, hm_recv, hm_cols, tail, u_full, m_cols, m_rows,
+               gain_ref, wo, wgu, wd, o_recv, p_send, p_recv, hm_send, hm_recv, hm_cols, tail, u_full, m_cols, m_rows,
                f_part, f_cols, f_send, f_recv,
                gain_sem, wo_sem, wgu_sem, wd_sem, os_sem, or_sem, ps_sem, pr_sem, hs_sem, hr_sem, fs_sem, fr_sem):
     y, x = position(ny, nx)
@@ -239,10 +237,11 @@
         wgu_copies[-1].start()
     wd_copy = pltpu.make_async_copy(wd_hbm, wd.at[pl.ds(0, ffn)], wd_sem)
     wd_copy.start()
-    barrier = greet_all(y, x, ny, nx)
+    others = peers(y, x, ny, nx)
+    barrier = greet_all(others)
     wd[ffn:, :] = jnp.zeros((wd.shape[0] - ffn, width), BF16)
     m_cols[ffn:, :] = jnp.zeros((m_cols.shape[0] - ffn, 128), F32)
-    f_part[many:, :] = jnp.zeros((f_part.shape[0] - many, width), F32)
+    f_part[many:, :] = jnp.zeros((f_part.shape[0] - many, f_part.shape[1]), F32)
     pl.semaphore_wait(barrier, total - 1)
 
     def o_copy(d):
@@ -257,31 +256,38 @@
     wo_copy.wait()
     o_rows = [jnp.concatenate([o_recv[t, h] for t in range(ny)], axis=0) for h in range(heads_y)]
     o_full = jnp.concatenate(o_rows, axis=1)
-    part[...] = lax.dot_general(o_full, wo[...], NN, preferred_element_type=F32)
-    for t in range(ny):
-        p_send[t] = part[rows * t:rows * (t + 1), :].astype(BF16)
-
-    def p_copy(d):
+    halves = ps_sem.shape[0]
+    wide = width // halves
+
+    def p_copy(c, d):
         py = (y + d) % ny
-        return remote(p_send.at[py], p_recv.at[y], ps_sem.at[d], pr_sem.at[d], py, x)
-
-    for d in range(1, ny):
-        p_copy(d).start()
-    p_recv[y] = p_send[y]
-    for d in range(1, ny):
-        p_copy(d).wait()
-    summed = p_recv[0].astype(F32)
-    for t in range(1, ny):
-        summed = summed + p_recv[t].astype(F32)
-    h_mid = (hrow_ref[...] + summed).astype(BF16)
-    hm_send[...] = h_mid
-
-    def h_copy(d):
+        at = pl.ds(c * wide, wide)
+        return remote(p_send.at[py, :, at], p_recv.at[y, :, at], ps_sem.at[c, d], pr_sem.at[c, d], py, x)
+
+    def h_copy(c, d):
         py = (y + d) % ny
-        return remote(hm_send, hm_recv.at[y], hs_sem.at[d], hr_sem.at[d], py, x)
-
-    for d in range(1, ny):
-        h_copy(d).start()
+        at = pl.ds(c * wide, wide)
+        return remote(hm_send.at[:, at], hm_recv.at[y, :, at], hs_sem.at[c, d], hr_sem.at[c, d], py, x)
+
+    for c in range(halves):
+        at = slice(c * wide, (c + 1) * wide)
+        part = lax.dot_general(o_full, wo[:, at], NN, preferred_element_type=F32).astype(BF16)
+        for t in range(ny):
+            p_send[t, :, at] = part[rows * t:rows * (t + 1)]
+        for d in (2, 1, 3):
+            p_copy(c, d).start()
+        p_recv[y, :, at] = p_send[y, :, at]
+    for c in range(halves):
+        at = slice(c * wide, (c + 1) * wide)
+        for d in range(1, ny):
+            p_copy(c, d).wait()
+        summed = p_recv[0, :, at].astype(F32)
+        for t in range(1, ny):
+            summed = summed + p_recv[t, :, at].astype(F32)
+        hm_send[:, at] = (hrow_ref[:, at] + summed).astype(BF16)
+        for d in (2, 1, 3):
+            h_copy(c, d).start()
+    h_mid = hm_send[...]
     hm_recv[y] = h_mid
 
     hm_cols[0:rows, :] = h_mid.astype(F32)
@@ -295,8 +301,9 @@
             corner = corner + lane_roll(f_cols[cols * s + 16 * k:cols * s + 16 * (k + 1), :], 64 + 16 * k)
         tail[s] = corner
 
-    for d in range(1, ny):
-        h_copy(d).wait()
+    for c in range(halves):
+        for d in range(1, ny):
+            h_copy(c, d).wait()
     gain_copy.wait()
     h64 = jnp.concatenate([hm_recv[t] for t in range(ny)], axis=0).astype(F32)
     inv = lax.rsqrt(jnp.sum(h64 * h64, axis=1, keepdims=True) / width + NORM_EPS)
@@ -317,34 +324,34 @@
     for j in range(m_rows.shape[1] // 128):
         m_rows[:, 128 * j:128 * (j + 1)] = jnp.transpose(m_cols[128 * j:128 * (j + 1), :])[0:many].astype(BF16)
     wd_copy.wait()
-    wide = 256
-    for n in range(width // wide):
-        f_part[0:many, wide * n:wide * (n + 1)] = lax.dot_general(
-            m_rows[...], wd[:, wide * n:wide * (n + 1)], NN, preferred_element_type=F32)
-    for j in range(width // 128):
-        f_cols[128 * j:128 * (j + 1), :] = jnp.transpose(f_part[:, 128 * j:128 * (j + 1)])
-    for s in range(total):
-        a0 = f_cols[cols * s:cols * s + 16, :]
-        a1 = f_cols[cols * s + 16:cols * s + 32, :]
-        a2 = lane_roll(f_cols[cols * s + 32:cols * s + 48, :], 64)
-        f_send[s, 0:16] = jnp.where(lane16 < 64, a0, a2).astype(BF16)
-        f_send[s, 16:32] = jnp.where(lane16 < 64, a1, tail[s]).astype(BF16)
-
-    def f_copy(d):
-        py, px = peer(y, x, d, ny, nx)
-        return remote(f_send.at[px * ny + py], f_recv.at[slot], fs_sem.at[d], fr_sem.at[d], py, px)
-
-    def f_start(d, carry):
-        f_copy(d).start()
-        return carry
-
-    def f_wait(d, carry):
-        f_copy(d).wait()
-        return carry
-
-    lax.fori_loop(1, total, f_start, 0)
+    group = 384 // cols
+    pair = group // ny
+    own = (x % pair) * ny + y
+    f_sends = []
+    for i in range(total // group):
+        c = (x // pair + 1 + i) % (total // group)
+        at = pl.ds(pl.multiple_of(c * 384, 384), 384)
+        f_part[0:many, :] = lax.dot_general(m_rows[...], wd[:, at], NN, preferred_element_type=F32)
+        for j in range(3):
+            f_cols[128 * j:128 * (j + 1), :] = jnp.transpose(f_part[:, 128 * j:128 * (j + 1)])
+        for s in range(group):
+            a0 = f_cols[cols * s:cols * s + 16, :]
+            a1 = f_cols[cols * s + 16:cols * s + 32, :]
+            a2 = lane_roll(f_cols[cols * s + 32:cols * s + 48, :], 64)
+            f_send[c * group + s, 0:16] = jnp.where(lane16 < 64, a0, a2).astype(BF16)
+            f_send[c * group + s, 16:32] = jnp.where(lane16 < 64, a1, tail[c * group + s]).astype(BF16)
+        last = i == total // group - 1
+        for k in range(1 if last else 0, group):
+            j = (own + k) % group
+            s = c * group + j
+            f_sends.append(remote(f_send.at[s], f_recv.at[slot], fs_sem.at[s], fr_sem.at[slot], j % ny, c * pair + j // ny))
+            f_sends[-1].start()
     f_recv[slot] = f_send[me]
-    lax.fori_loop(1, total, f_wait, 0)
+    for copy in f_sends:
+        copy.wait_send()
+    for k in range(1, total):
+        s = (slot + k) % total
+        remote(f_send.at[s], f_recv.at[s], fs_sem.at[s], fr_sem.at[s], (y + 1) % ny, x).wait_recv()
 
     sums = [[jnp.zeros((16, 128), F32) for _ in range(3)] for _ in range(ny)]
     olds = [[jnp.zeros((16, 128), F32) for _ in range(3)] for _ in range(ny)]
@@ -415,7 +422,7 @@
             in_specs=[pl.BlockSpec(memory_space=pltpu.SMEM), vmem, vmem, vmem],
             out_specs=(hbm, hbm, vmem, vmem, vmem),
             input_output_aliases={2: 3, 3: 4},
-            scratch_shapes=[pltpu.VMEM((2, 16, slots), F32), pltpu.VMEM((rows, 16, head_dim), F32), dma((rows,)), dma((rows,))],
+            scratch_shapes=[pltpu.VMEM((2, 32, slots), F32), pltpu.VMEM((rows, 16, head_dim), F32), dma((rows,)), dma((rows,))],
             compiler_params=pltpu.CompilerParams(vmem_limit_bytes=8 << 20),
             cost_estimate=pl.CostEstimate(flops=8_000_000_000, bytes_accessed=20_000_000, transcendentals=0),
             name='attend',
@@ -429,14 +436,15 @@
             scratch_shapes=[
                 pltpu.VMEM(mlp_gain.shape, BF16),
                 pltpu.VMEM(w_out.shape, BF16), pltpu.VMEM(w_gate_up.shape, BF16), pltpu.VMEM((ffn_pad, width), BF16),
-                pltpu.VMEM((ny, heads // ny, rows, head_dim), BF16), pltpu.VMEM((many, width), F32),
+                pltpu.VMEM((ny, heads // ny, rows, head_dim), BF16),
                 pltpu.VMEM((ny, rows, width), BF16), pltpu.VMEM((ny, rows, width), BF16),
                 pltpu.VMEM((rows, width), BF16), pltpu.VMEM((ny, rows, width), BF16),
                 pltpu.VMEM((128, width), F32), pltpu.VMEM((total, 16, 128), F32),
                 pltpu.VMEM((many, width), BF16), pltpu.VMEM((ffn_pad, 128), F32), pltpu.VMEM((many, ffn_pad), BF16),
-                pltpu.VMEM((128, width), F32), pltpu.VMEM((width, 128), F32),
+                pltpu.VMEM((128, 384), F32), pltpu.VMEM((width, 128), F32),
                 pltpu.VMEM((total, 32, 128), BF16), pltpu.VMEM((total, 32, 128), BF16),
-                dma, dma, dma((chunk,)), dma, dma((ny,)), dma((ny,)), dma((ny,)), dma((ny,)), dma((ny,)), dma((ny,)),
+                dma, dma, dma((chunk,)), dma, dma((ny,)), dma((ny,)),
+                dma((2, ny)), dma((2, ny)), dma((2, ny)), dma((2, ny)),
                 dma((total,)), dma((total,))],
             compiler_params=pltpu.CompilerParams(collective_id=1, has_side_effects=True, vmem_limit_bytes=44 << 20),
             name='mlp',

time: 63 us -> 59.5 us (0.944)
  Pallas kernels: 61.6 us -> 58.1 us
    pallas_call x1, Pallas kernels: 11.3 us -> 10 us  [layer(): pl.pallas_call(functools.partial(attend_kernel, heads, head_dim ** (-0.5)...]
    pallas_call x1, Pallas kernels: 30.4 us -> 29.2 us  [layer(): pl.pallas_call(functools.partial(mlp_kernel, ny, nx, cols, rows, width, h...]
    pallas_call x1, Pallas kernels: 20 us -> 18.9 us  [layer(): pl.pallas_call(functools.partial(qkv_kernel, ny, nx, cols, rows, width),...]
where the time goes in v3:
time: 59.5 us; the launch traced here: 59.4 us
  Pallas kernels  58.1 us (98%)
  between operations  0.67 us (1%)
  local copies, waits for them, and re-layouts  0.63 us (1%)
    pallas_call x1, Pallas kernels, layer(): pl.pallas_call(functools.partial(mlp_kernel, ny, nx, cols, rows, width, h...  29.2 us
    pallas_call x1, Pallas kernels, layer(): pl.pallas_call(functools.partial(qkv_kernel, ny, nx, cols, rows, width),...  18.9 us
    pallas_call x1, Pallas kernels, layer(): pl.pallas_call(functools.partial(attend_kernel, heads, head_dim ** (-0.5)...  10 us

profile of v3, /device:TPU:97, one launch (start us, length us, event | category | flops | bytes accessed | tf_op | source)
XLA Modules:
  0.0 59.4 jit_solution(13761253067730329335)
XLA Ops:
  0.6 0.0 copy-start
  0.6 18.9 %qkv.1 = (f32[16,16,128]{2,1,0:T(8,128)S(1)}, f32[16,1536]{1,0:T(8,128)S(1)}, bf16[16,2048,128]{2,1,0:T(8,128)(2,1)S(1)}, bf16[16,2048,128]{2,1,0:T(8,128)(2,1)S(1)}) custom-call(bf16[48,512]{1,0:T(8,128)(2,1)} %bitcast.21, bf16[1,1536]{1,0:T(2,128)(2,1)} %gain_hbm.2, bf16[448,1536]{1,0:T(8,128)(2,1)} %bitcast.20, bf16[16,2048,128]{2,1,0:T(8,128)(2,1)} %bitcast.18, ...), custom_call_target="tpu_custom_call" | custom-call | flops 8000000000 | bytes 20000000 | tf_op jit(solution)/shard_map/qkv/pallas_call | solution.py:400
  19.6 0.0 copy-done
  19.6 10.0 %attend.1 = (bf16[16,2048,128]{2,1,0:T(8,128)(2,1)}, bf16[16,2048,128]{2,1,0:T(8,128)(2,1)}, bf16[12,16,128]{2,1,0:T(8,128)(2,1)S(1)}, bf16[16,2048,128]{2,1,0:T(8,128)(2,1)S(1)}, bf16[16,2048,128]{2,1,0:T(8,128)(2,1)S(1)}) custom-call(s32[16]{0:T(128)S(1)} %copy-done, ...), custom_call_target="tpu_custom_call", output_to_operand_aliasing={{3}: (2, {}), {4}: (3, {})} | custom-call | flops 8000000000 | bytes 20000000 | tf_op jit(solution)/shard_map/attend/pallas_call | solution.py:417
  29.6 29.2 %mlp.1 = bf16[48,512]{1,0:T(8,128)(2,1)S(1)} custom-call(bf16[12,16,128]{2,1,0:T(8,128)(2,1)S(1)} %get-tuple-element.13.o_ref, f32[16,1536]{1,0:T(8,128)S(1)} %get-tuple-element.14.hrow_ref, bf16[1,1536]{1,0:T(2,128)(2,1)} %gain_hbm.3, bf16[384,1536]{1,0:T(8,128)(2,1)} %bitcast.17, bf16[2,2240,1536]{2,1,0:T(8,128)(2,1)} %bitcast.15, bf16[2240,1536]{1,0:T(8,128)(2,1)} %bitcast.16), custom_call_target="tpu_custom_call" | custom-call | tf_op jit(solution)/shard_map/mlp/pallas_call | solution.py:431
  58.8 0.6 %copy.18 = bf16[512,48]{0,1:T(8,128)(2,1)} copy(bf16[512,48]{0,1:T(8,128)(2,1)S(1)} %bitcast.14) | data formatting | bytes 98304
Async XLA Ops:
  0.6 18.9 %copy-start = (s32[16]{0:T(128)S(1)}, s32[16]{0:T(128)}, u32[]{:S(2)}) copy-start(s32[16]{0:T(128)} %len_ref.1) | copy-start | bytes 196

commit v4 on v3

--- a/solution.py
+++ b/solution.py
@@ -173,15 +173,15 @@
         v_copy(b).start()
         return carry
 
-    def score(i):
+    def score(i, slot):
         blank = jnp.zeros((16, 128), BF16)
         q0, q1 = z_ref[2 * i].astype(BF16), z_ref[2 * i + 1].astype(BF16)
         q = jnp.concatenate([jnp.concatenate([q0, blank], axis=1), jnp.concatenate([blank, q1], axis=1)], axis=0)
         keys = jnp.concatenate([k_ref[2 * i], k_ref[2 * i + 1]], axis=1)
-        s_buf[i % 2] = lax.dot_general(q, keys, NT, preferred_element_type=F32) * scale
-
-    def finish(i):
-        s = s_buf[i % 2]
+        s_buf[slot] = lax.dot_general(q, keys, NT, preferred_element_type=F32) * scale
+
+    def finish(i, slot):
+        s = s_buf[slot]
         first = lax.broadcasted_iota(jnp.int32, (32, 1), 0) < 16
         length = jnp.where(first, len_ref[2 * i], len_ref[2 * i + 1])
         s = jnp.where(lane_ids(s.shape) <= length, s, -1e30)
@@ -194,15 +194,11 @@
 
     lax.fori_loop(0, rows, place, 0)
     lax.fori_loop(0, rows, leave, 0)
-    score(0)
-
-    def step(i, carry):
-        score(i + 1)
-        finish(i)
-        return carry
-
-    lax.fori_loop(0, rows // 2 - 1, step, 0)
-    finish(rows // 2 - 1)
+    score(0, 0)
+    for i in range(rows // 2 - 1):
+        score(i + 1, (i + 1) % 2)
+        finish(i, i % 2)
+    finish(rows // 2 - 1, (rows // 2 - 1) % 2)
     for h in range(heads):
         o_ref[h] = o_acc[:, h, :].astype(BF16)
 
@@ -214,141 +210,141 @@
     lax.fori_loop(0, rows, drain, 0)
 
 
-def mlp_kernel(ny, nx, cols, rows, width, heads, o_ref, hrow_ref, gain_hbm, wo_hbm, wgu_hbm, wd_hbm, out_ref,
-               gain_ref, wo, wgu, wd, o_recv, p_send, p_recv, hm_send, hm_recv, hm_cols, tail, u_full, m_cols, m_rows,
-               f_part, f_cols, f_send, f_recv,
-               gain_sem, wo_sem, wgu_sem, wd_sem, os_sem, or_sem, ps_sem, pr_sem, hs_sem, hr_sem, fs_sem, fr_sem):
-    y, x = position(ny, nx)
+def proj_kernel(ny, nx, cols, rows, width, heads, o_ref, hrow_ref, gain_hbm, wo_hbm, wgu_hbm, wd_hbm,
+                u_ref, tail_ref, wgu_ref, wd_ref,
+                gain_ref, wo, o_recv, p_send, p_recv, hm_send, hm_recv, hm_rows, hm_cols,
+                gain_sem, wo_sem, wgu_sem, wd_sem, os_sem, or_sem, ps_sem, pr_sem, hs_sem, hr_sem):
+    y, x = lax.axis_index('yz'), lax.axis_index('x')
     total = ny * nx
-    me = x * ny + y
-    slot = y * nx + x
     heads_y = heads // ny
     many = ny * rows
-    ffn = wgu_hbm.shape[1]
-    chunk = wgu_sem.shape[0]
-    step = ffn // chunk
+    ffn = wd_hbm.shape[0]
+    ring = [(d, (y + d) % ny) for d in sorted(range(1, ny), key=lambda d: -min(d, ny - d))]
+    barrier = pltpu.get_barrier_semaphore()
+    for _, py in ring:
+        pl.semaphore_signal(barrier, inc=1, device_id={'yz': py, 'x': x}, device_id_type=MESH)
+    wo_copy = pltpu.make_async_copy(wo_hbm, wo, wo_sem)
     gain_copy = pltpu.make_async_copy(gain_hbm, gain_ref, gain_sem)
-    gain_copy.start()
-    wo_copy = pltpu.make_async_copy(wo_hbm, wo, wo_sem)
-    wo_copy.start()
-    wgu_copies = []
-    for c in range(chunk):
-        wgu_copies.append(pltpu.make_async_copy(wgu_hbm.at[:, pl.ds(c * step, step)], wgu.at[:, pl.ds(c * step, step)], wgu_sem.at[c]))
-        wgu_copies[-1].start()
-    wd_copy = pltpu.make_async_copy(wd_hbm, wd.at[pl.ds(0, ffn)], wd_sem)
-    wd_copy.start()
-    others = peers(y, x, ny, nx)
-    barrier = greet_all(others)
-    wd[ffn:, :] = jnp.zeros((wd.shape[0] - ffn, width), BF16)
-    m_cols[ffn:, :] = jnp.zeros((m_cols.shape[0] - ffn, 128), F32)
-    f_part[many:, :] = jnp.zeros((f_part.shape[0] - many, f_part.shape[1]), F32)
-    pl.semaphore_wait(barrier, total - 1)
-
-    def o_copy(d):
-        py = (y + d) % ny
-        return remote(o_ref.at[pl.ds(py * heads_y, heads_y)], o_recv.at[y], os_sem.at[d], or_sem.at[d], py, x)
-
-    for d in range(1, ny):
-        o_copy(d).start()
+    parts = wgu_sem.shape[0]
+    share = ffn // parts
+    loads = [pltpu.make_async_copy(wgu_hbm.at[:, pl.ds(c * share, share)], wgu_ref.at[:, pl.ds(c * share, share)], wgu_sem.at[c])
+             for c in range(parts)]
+    loads.append(pltpu.make_async_copy(wd_hbm, wd_ref.at[pl.ds(0, ffn)], wd_sem))
+    for copy in [wo_copy, gain_copy] + loads:
+        copy.start()
+    pl.semaphore_wait(barrier, ny - 1)
+
+    o_sends = [remote(o_ref.at[pl.ds(py * heads_y, heads_y)], o_recv.at[y], os_sem.at[d], or_sem.at[d], py, x) for d, py in ring]
+    for copy in o_sends:
+        copy.start()
     o_recv[y] = o_ref[pl.ds(y * heads_y, heads_y)]
-    for d in range(1, ny):
-        o_copy(d).wait()
+    wd_ref[ffn:, :] = jnp.zeros((wd_ref.shape[0] - ffn, width), BF16)
     wo_copy.wait()
+    for copy in o_sends:
+        copy.wait()
     o_rows = [jnp.concatenate([o_recv[t, h] for t in range(ny)], axis=0) for h in range(heads_y)]
     o_full = jnp.concatenate(o_rows, axis=1)
+
     halves = ps_sem.shape[0]
     wide = width // halves
 
-    def p_copy(c, d):
-        py = (y + d) % ny
+    def p_copies(c):
         at = pl.ds(c * wide, wide)
-        return remote(p_send.at[py, :, at], p_recv.at[y, :, at], ps_sem.at[c, d], pr_sem.at[c, d], py, x)
-
-    def h_copy(c, d):
-        py = (y + d) % ny
+        return [remote(p_send.at[py, :, at], p_recv.at[y, :, at], ps_sem.at[c, d], pr_sem.at[c, d], py, x) for d, py in ring]
+
+    def h_copies(c):
         at = pl.ds(c * wide, wide)
-        return remote(hm_send.at[:, at], hm_recv.at[y, :, at], hs_sem.at[c, d], hr_sem.at[c, d], py, x)
+        return [remote(hm_send.at[:, at], hm_recv.at[y, :, at], hs_sem.at[c, d], hr_sem.at[c, d], py, x) for d, py in ring]
 
     for c in range(halves):
         at = slice(c * wide, (c + 1) * wide)
         part = lax.dot_general(o_full, wo[:, at], NN, preferred_element_type=F32).astype(BF16)
         for t in range(ny):
             p_send[t, :, at] = part[rows * t:rows * (t + 1)]
-        for d in (2, 1, 3):
-            p_copy(c, d).start()
+        for copy in p_copies(c):
+            copy.start()
         p_recv[y, :, at] = p_send[y, :, at]
     for c in range(halves):
         at = slice(c * wide, (c + 1) * wide)
-        for d in range(1, ny):
-            p_copy(c, d).wait()
+        for copy in p_copies(c):
+            copy.wait()
         summed = p_recv[0, :, at].astype(F32)
         for t in range(1, ny):
             summed = summed + p_recv[t, :, at].astype(F32)
         hm_send[:, at] = (hrow_ref[:, at] + summed).astype(BF16)
-        for d in (2, 1, 3):
-            h_copy(c, d).start()
+        for copy in h_copies(c):
+            copy.start()
     h_mid = hm_send[...]
     hm_recv[y] = h_mid
 
-    hm_cols[0:rows, :] = h_mid.astype(F32)
-    hm_cols[rows:, :] = jnp.zeros((hm_cols.shape[0] - rows, width), F32)
+    hm_rows[0:rows, :] = h_mid.astype(F32)
+    hm_rows[rows:, :] = jnp.zeros((hm_rows.shape[0] - rows, width), F32)
     for j in range(width // 128):
-        f_cols[128 * j:128 * (j + 1), :] = jnp.transpose(hm_cols[:, 128 * j:128 * (j + 1)])
-    lane16 = lane_ids((16, 128))
+        hm_cols[128 * j:128 * (j + 1), :] = jnp.transpose(hm_rows[:, 128 * j:128 * (j + 1)])
     for s in range(total):
         corner = jnp.zeros((16, 128), F32)
         for k in range(cols // 16):
-            corner = corner + lane_roll(f_cols[cols * s + 16 * k:cols * s + 16 * (k + 1), :], 64 + 16 * k)
-        tail[s] = corner
-
+            corner = corner + lane_roll(hm_cols[cols * s + 16 * k:cols * s + 16 * (k + 1), :], 64 + 16 * k)
+        tail_ref[s] = corner
+    u_ref[many:, :] = jnp.zeros((u_ref.shape[0] - many, width), BF16)
+
+    gain_copy.wait()
     for c in range(halves):
-        for d in range(1, ny):
-            h_copy(c, d).wait()
-    gain_copy.wait()
+        for copy in h_copies(c):
+            copy.wait()
     h64 = jnp.concatenate([hm_recv[t] for t in range(ny)], axis=0).astype(F32)
     inv = lax.rsqrt(jnp.sum(h64 * h64, axis=1, keepdims=True) / width + NORM_EPS)
-    u_full[...] = (h64 * inv * gain_ref[...].astype(F32)).astype(BF16)
-
-    def gate_up(c, carry):
-        at = pl.multiple_of(c * step, step)
-        pltpu.make_async_copy(wgu_hbm.at[:, pl.ds(at, step)], wgu.at[:, pl.ds(at, step)], wgu_sem.at[c]).wait()
-        gate = lax.dot_general(wgu[0, pl.ds(at, step), :], u_full[...], NT, preferred_element_type=F32)
-        up = lax.dot_general(wgu[1, pl.ds(at, step), :], u_full[...], NT, preferred_element_type=F32)
+    u_ref[0:many, :] = (h64 * inv * gain_ref[...].astype(F32)).astype(BF16)
+    for copy in loads:
+        copy.wait()
+
+
+def mlp_kernel(ny, nx, cols, rows, width, ffn, u_ref, tail_ref, wgu, wd, out_ref, m_rows, f_part, f_cols, f_send, f_recv, fs_sem, fr_sem):
+    y, x = lax.axis_index('yz'), lax.axis_index('x')
+    total = ny * nx
+    me = x * ny + y
+    slot = y * nx + x
+    many = ny * rows
+    barrier = greet_all(peers(y, x, ny, nx))
+    lane16 = lane_ids((16, 128))
+
+    for base in range(0, ffn, 512):
+        size = min(512, ffn - base)
+        gate = lax.dot_general(wgu[0, base:base + size, :], u_ref[...], NT, preferred_element_type=F32)
+        up = lax.dot_general(wgu[1, base:base + size, :], u_ref[...], NT, preferred_element_type=F32)
         gate = gate.astype(BF16).astype(F32)
-        up = up.astype(BF16).astype(F32)
-        m_cols[pl.ds(at, step), 0:many] = jax.nn.silu(gate) * up
-        return carry
-
-    m_cols[:, many:] = jnp.zeros((m_cols.shape[0], 128 - many), F32)
-    lax.fori_loop(0, chunk, gate_up, 0)
-    for j in range(m_rows.shape[1] // 128):
-        m_rows[:, 128 * j:128 * (j + 1)] = jnp.transpose(m_cols[128 * j:128 * (j + 1), :])[0:many].astype(BF16)
-    wd_copy.wait()
-    group = 384 // cols
-    pair = group // ny
-    own = (x % pair) * ny + y
+        m = jax.nn.silu(gate) * up.astype(BF16).astype(F32)
+        if size % 128:
+            m = jnp.concatenate([m, jnp.zeros((128 - size % 128, 128), F32)], axis=0)
+        for j in range(m.shape[0] // 128):
+            m_rows[:, base + 128 * j:base + 128 * (j + 1)] = jnp.transpose(m[128 * j:128 * (j + 1)])[0:many].astype(BF16)
+
+    chunks = f_part.shape[0]
+    wide = width // chunks
+    group = total // chunks
+    span = nx // chunks
+    own = (x % span) * ny + y
+    f_part[:, many:, :] = jnp.zeros((chunks, f_part.shape[1] - many, wide), F32)
+    pl.semaphore_wait(barrier, total - 1)
     f_sends = []
-    for i in range(total // group):
-        c = (x // pair + 1 + i) % (total // group)
-        at = pl.ds(pl.multiple_of(c * 384, 384), 384)
-        f_part[0:many, :] = lax.dot_general(m_rows[...], wd[:, at], NN, preferred_element_type=F32)
-        for j in range(3):
-            f_cols[128 * j:128 * (j + 1), :] = jnp.transpose(f_part[:, 128 * j:128 * (j + 1)])
+    for i in range(chunks):
+        c = (x // span + 1 + i) % chunks
+        at = pl.ds(pl.multiple_of(c * wide, wide), wide)
+        f_part[i, 0:many, :] = lax.dot_general(m_rows[...], wd[:, at], NN, preferred_element_type=F32)
+        for j in range(wide // 128):
+            f_cols[i, 128 * j:128 * (j + 1), :] = jnp.transpose(f_part[i, :, 128 * j:128 * (j + 1)])
         for s in range(group):
-            a0 = f_cols[cols * s:cols * s + 16, :]
-            a1 = f_cols[cols * s + 16:cols * s + 32, :]
-            a2 = lane_roll(f_cols[cols * s + 32:cols * s + 48, :], 64)
+            a0 = f_cols[i, cols * s:cols * s + 16, :]
+            a1 = f_cols[i, cols * s + 16:cols * s + 32, :]
+            a2 = lane_roll(f_cols[i, cols * s + 32:cols * s + 48, :], 64)
             f_send[c * group + s, 0:16] = jnp.where(lane16 < 64, a0, a2).astype(BF16)
-            f_send[c * group + s, 16:32] = jnp.where(lane16 < 64, a1, tail[c * group + s]).astype(BF16)
-        last = i == total // group - 1
-        for k in range(1 if last else 0, group):
+            f_send[c * group + s, 16:32] = jnp.where(lane16 < 64, a1, tail_ref[c * group + s]).astype(BF16)
+        for k in range(1 if i == chunks - 1 else 0, group):
             j = (own + k) % group
             s = c * group + j
-            f_sends.append(remote(f_send.at[s], f_recv.at[slot], fs_sem.at[s], fr_sem.at[slot], j % ny, c * pair + j // ny))
+            f_sends.append(remote(f_send.at[s], f_recv.at[slot], fs_sem.at[s], fr_sem.at[slot], j % ny, c * span + j // ny))
             f_sends[-1].start()
     f_recv[slot] = f_send[me]
-    for copy in f_sends:
-        copy.wait_send()
     for k in range(1, total):
         s = (slot + k) % total
         remote(f_send.at[s], f_recv.at[s], fs_sem.at[s], fr_sem.at[s], (y + 1) % ny, x).wait_recv()
@@ -372,6 +368,8 @@
     for t in range(ny):
         for k in range(3):
             out_ref[16 * k:16 * (k + 1), 128 * t:128 * (t + 1)] = (olds[t][k] + sums[t][k]).astype(BF16)
+    for copy in f_sends:
+        copy.wait_send()
 
 
 def solution(mesh):
@@ -427,28 +425,36 @@
             cost_estimate=pl.CostEstimate(flops=8_000_000_000, bytes_accessed=20_000_000, transcendentals=0),
             name='attend',
         )(seq_lens, z, k_vmem, v_vmem)
-        chunk = 5
-        out = pl.pallas_call(
-            functools.partial(mlp_kernel, ny, nx, cols, rows, width, heads),
-            out_shape=jax.ShapeDtypeStruct(ht.shape, BF16),
+        u, tail, wgu_vmem, wd_vmem = pl.pallas_call(
+            functools.partial(proj_kernel, ny, nx, cols, rows, width, heads),
+            out_shape=(pltpu.VMEM((128, width), BF16), pltpu.VMEM((total, 16, 128), F32),
+                       pltpu.VMEM(w_gate_up.shape, BF16), pltpu.VMEM((ffn_pad, width), BF16)),
             in_specs=[vmem, vmem, hbm, hbm, hbm, hbm],
-            out_specs=vmem,
+            out_specs=(vmem,) * 4,
             scratch_shapes=[
-                pltpu.VMEM(mlp_gain.shape, BF16),
-                pltpu.VMEM(w_out.shape, BF16), pltpu.VMEM(w_gate_up.shape, BF16), pltpu.VMEM((ffn_pad, width), BF16),
+                pltpu.VMEM(mlp_gain.shape, BF16), pltpu.VMEM(w_out.shape, BF16),
                 pltpu.VMEM((ny, heads // ny, rows, head_dim), BF16),
                 pltpu.VMEM((ny, rows, width), BF16), pltpu.VMEM((ny, rows, width), BF16),
                 pltpu.VMEM((rows, width), BF16), pltpu.VMEM((ny, rows, width), BF16),
-                pltpu.VMEM((128, width), F32), pltpu.VMEM((total, 16, 128), F32),
-                pltpu.VMEM((many, width), BF16), pltpu.VMEM((ffn_pad, 128), F32), pltpu.VMEM((many, ffn_pad), BF16),
-                pltpu.VMEM((128, 384), F32), pltpu.VMEM((width, 128), F32),
-                pltpu.VMEM((total, 32, 128), BF16), pltpu.VMEM((total, 32, 128), BF16),
-                dma, dma, dma((chunk,)), dma, dma((ny,)), dma((ny,)),
-                dma((2, ny)), dma((2, ny)), dma((2, ny)), dma((2, ny)),
-                dma((total,)), dma((total,))],
-            compiler_params=pltpu.CompilerParams(collective_id=1, has_side_effects=True, vmem_limit_bytes=44 << 20),
+                pltpu.VMEM((128, width), F32), pltpu.VMEM((width, 128), F32),
+                dma, dma, dma((5,)), dma, dma((ny,)), dma((ny,)),
+                dma((2, ny)), dma((2, ny)), dma((2, ny)), dma((2, ny))],
+            compiler_params=pltpu.CompilerParams(collective_id=1, has_side_effects=True, vmem_limit_bytes=12 << 20),
+            cost_estimate=pl.CostEstimate(flops=8_000_000_000, bytes_accessed=20_000_000, transcendentals=0),
+            name='proj',
+        )(o, hrow, in_hbm(mlp_gain), in_hbm(w_out), in_hbm(w_gate_up), in_hbm(w_down))
+        out = pl.pallas_call(
+            functools.partial(mlp_kernel, ny, nx, cols, rows, width, ffn),
+            out_shape=jax.ShapeDtypeStruct(ht.shape, BF16),
+            in_specs=[vmem] * 4,
+            out_specs=vmem,
+            scratch_shapes=[
+                pltpu.VMEM((many, ffn_pad), BF16), pltpu.VMEM((2, 128, width // 2), F32), pltpu.VMEM((2, width // 2, 128), F32),
+                pltpu.VMEM((total, 32, 128), BF16), pltpu.VMEM((total, 32, 128), BF16), dma((total,)), dma((total,))],
+            compiler_params=pltpu.CompilerParams(collective_id=2, has_side_effects=True, vmem_limit_bytes=12 << 20),
+            cost_estimate=pl.CostEstimate(flops=8_000_000_000, bytes_accessed=20_000_000, transcendentals=0),
             name='mlp',
-        )(o, hrow, in_hbm(mlp_gain), in_hbm(w_out), in_hbm(w_gate_up), in_hbm(w_down))
+        )(u, tail, wgu_vmem, wd_vmem)
         return out, k_new, v_new
 
     def local_step(hidden, seq_lens, attn_gain, mlp_gain, w_qkv, w_out, w_gate_up, w_down, k_cache, v_cache):

time: 59.5 us -> 55 us (0.924)
  Pallas kernels: 58.1 us -> 53.6 us
    pallas_call x1, Pallas kernels: 10 us -> 6.89 us  [layer(): pl.pallas_call(functools.partial(attend_kernel, heads, head_dim ** (-0.5)...]
    pallas_call x1 -> x2, Pallas kernels: 29.2 us -> 27.8 us  [the longest x1 16.1 us: layer(): pl.pallas_call(functools.partial(mlp_kernel, ny, nx, cols, rows, width, f...]
where the time goes in v4:
time: 55 us; the launch traced here: 54.9 us
  Pallas kernels  53.6 us (97%)
  between operations  0.68 us (1%)
  local copies, waits for them, and re-layouts  0.63 us (1%)
    pallas_call x1, Pallas kernels, layer(): pl.pallas_call(functools.partial(qkv_kernel, ny, nx, cols, rows, width),...  18.9 us
    pallas_call x1, Pallas kernels, layer(): pl.pallas_call(functools.partial(mlp_kernel, ny, nx, cols, rows, width, f...  16.1 us
    pallas_call x1, Pallas kernels, layer(): pl.pallas_call(functools.partial(proj_kernel, ny, nx, cols, rows, width,...  11.6 us
    pallas_call x1, Pallas kernels, layer(): pl.pallas_call(functools.partial(attend_kernel, heads, head_dim ** (-0.5)...  6.89 us

profile of v4, /device:TPU:97, one launch (start us, length us, event | category | flops | bytes accessed | tf_op | source)
XLA Modules:
  0.0 54.9 jit_solution(5929298623295496820)
XLA Ops:
  0.6 0.0 copy-start
  0.6 18.9 %qkv.1 = (f32[16,16,128]{2,1,0:T(8,128)S(1)}, f32[16,1536]{1,0:T(8,128)S(1)}, bf16[16,2048,128]{2,1,0:T(8,128)(2,1)S(1)}, bf16[16,2048,128]{2,1,0:T(8,128)(2,1)S(1)}) custom-call(bf16[48,512]{1,0:T(8,128)(2,1)} %bitcast.21, bf16[1,1536]{1,0:T(2,128)(2,1)} %gain_hbm.2, bf16[448,1536]{1,0:T(8,128)(2,1)} %bitcast.19, bf16[16,2048,128]{2,1,0:T(8,128)(2,1)} %bitcast.16, ...), custom_call_target="tpu_custom_call" | custom-call | flops 8000000000 | bytes 20000000 | tf_op jit(solution)/shard_map/qkv/pallas_call | solution.py:398
  19.6 0.0 copy-done
  19.6 6.9 %attend.1 = (bf16[16,2048,128]{2,1,0:T(8,128)(2,1)}, bf16[16,2048,128]{2,1,0:T(8,128)(2,1)}, bf16[12,16,128]{2,1,0:T(8,128)(2,1)S(1)}, bf16[16,2048,128]{2,1,0:T(8,128)(2,1)S(1)}, bf16[16,2048,128]{2,1,0:T(8,128)(2,1)S(1)}) custom-call(s32[16]{0:T(128)S(1)} %copy-done, ...), custom_call_target="tpu_custom_call", output_to_operand_aliasing={{3}: (2, {}), {4}: (3, {})} | custom-call | flops 8000000000 | bytes 20000000 | tf_op jit(solution)/shard_map/attend/pallas_call | solution.py:415
  26.5 11.6 %proj.1 = (bf16[128,1536]{1,0:T(8,128)(2,1)S(1)}, f32[32,16,128]{2,1,0:T(8,128)S(1)}, bf16[2,2240,1536]{2,1,0:T(8,128)(2,1)S(1)}, bf16[2304,1536]{1,0:T(8,128)(2,1)S(1)}) custom-call(bf16[12,16,128]{2,1,0:T(8,128)(2,1)S(1)} %get-tuple-element.17.o_ref, f32[16,1536]{1,0:T(8,128)S(1)} %get-tuple-element.18.hrow_ref, bf16[1,1536]{1,0:T(2,128)(2,1)} %gain_hbm.3, ...), custom_call_target="tpu_custom_call" | custom-call | flops 8000000000 | bytes 20000000 | tf_op jit(solution)/shard_map/proj/pallas_call | solution.py:428
  38.1 16.1 %mlp.1 = bf16[48,512]{1,0:T(8,128)(2,1)S(1)} custom-call(bf16[128,1536]{1,0:T(8,128)(2,1)S(1)} %get-tuple-element.19.u_ref, f32[32,16,128]{2,1,0:T(8,128)S(1)} %get-tuple-element.20.tail_ref, bf16[2,2240,1536]{2,1,0:T(8,128)(2,1)S(1)} %get-tuple-element.21.wgu, bf16[2304,1536]{1,0:T(8,128)(2,1)S(1)} %get-tuple-element.22.wd), custom_call_target="tpu_custom_call" | custom-call | flops 8000000000 | bytes 20000000 | tf_op jit(solution)/shard_map/mlp/pallas_call | solution.py:446
  54.3 0.6 %copy.18 = bf16[512,48]{0,1:T(8,128)(2,1)} copy(bf16[512,48]{0,1:T(8,128)(2,1)S(1)} %bitcast.14) | data formatting | bytes 98304
Async XLA Ops:
  0.6 18.9 %copy-start = (s32[16]{0:T(128)S(1)}, s32[16]{0:T(128)}, u32[]{:S(2)}) copy-start(s32[16]{0:T(128)} %len_ref.1) | copy-start | bytes 196

commit v5 on v4

--- a/solution.py
+++ b/solution.py
@@ -24,8 +24,9 @@
     return v if shift == 0 else pltpu.roll(v, shift, v.ndim - 1)
 
 
-def position(ny, nx):
-    return lax.axis_index('yz'), lax.axis_index('x')
+def twist(t, g, ny):
+    flip = (t // (ny // 2)) % 2
+    return g + flip * (1 - 2 * (g % 2))
 
 
 def peers(y, x, ny, nx):
@@ -36,6 +37,11 @@
     return [(dy * nx + dx, ys[dy], xs[dx]) for dx in far_x for dy in far_y if dy or dx]
 
 
+def ring(y, g, ny):
+    far = sorted(range(1, ny), key=lambda d: -min(d, ny - d))
+    return [(d, (y + d) % ny, twist((y + d) % ny, g, ny)) for d in far]
+
+
 def greet_all(others):
     barrier = pltpu.get_barrier_semaphore()
     for _, py, px in others:
@@ -51,7 +57,8 @@
 def qkv_kernel(ny, nx, cols, rows, width, ht_hbm, gain_hbm, w_hbm, k_hbm, v_hbm, z_ref, hrow_ref, k_ref, v_ref,
                ht_ref, gain_ref, send_buf, recv_buf, w_vmem, gain_col, h_full, u_full, zt_buf, z_send, z_recv, h_rows,
                h_sem, g_sem, w_sem, kv_sem, send_sem, recv_sem, zsend_sem, zrecv_sem):
-    y, x = position(ny, nx)
+    y, x = lax.axis_index('yz'), lax.axis_index('x')
+    mine = twist(y, x, ny)
     total = ny * nx
     me = x * ny + y
     qcols = w_hbm.shape[0]
@@ -73,22 +80,23 @@
 
     lane = lane_ids((cols, 128))
     lane16 = lane_ids((16, 128))
+    half = cols // 2
     tiles = [ht_ref[:, 128 * t:128 * (t + 1)].astype(F32) for t in range(ny)]
-    for px in range(nx):
+    for g in range(nx):
         block = jnp.zeros((cols, 128), F32)
         for t in range(ny):
-            piece = lane_roll(tiles[t], rows * t - rows * px)
+            piece = lane_roll(tiles[t], rows * t - rows * twist(t, g, ny))
             block = jnp.where((lane >= rows * t) & (lane < rows * (t + 1)), piece, block)
-        high = lane_roll(block[32:48], 64)
-        send_buf[px, 0:16] = jnp.where(lane16 < 64, block[0:16], high).astype(BF16)
-        send_buf[px, 16:32] = block[16:32].astype(BF16)
+        block = jnp.where(lane[0:half] < 64, block[0:half], lane_roll(block[half:cols], 64))
+        for k in range(half // 8):
+            send_buf[g, k] = block[8 * k:8 * (k + 1)].astype(BF16)
 
     pl.semaphore_wait(barrier, total - 1)
 
-    h_sends = [remote(send_buf.at[px], recv_buf.at[me], send_sem.at[d], recv_sem.at[d], py, px) for d, py, px in others]
+    h_sends = [remote(send_buf.at[twist(py, px, ny)], recv_buf.at[me], send_sem.at[d], recv_sem.at[d], py, px) for d, py, px in others]
     for copy in h_sends:
         copy.start()
-    recv_buf[me] = send_buf[x]
+    recv_buf[me] = send_buf[mine]
 
     g_copy.wait()
     for j in range(width // 128):
@@ -99,15 +107,14 @@
     for copy in h_sends:
         copy.wait()
 
-    square = jnp.zeros((16, 128), F32)
+    square = jnp.zeros((8, 128), F32)
     for s in range(total):
-        low = recv_buf[s, 0:16].astype(F32)
-        mid = recv_buf[s, 16:32].astype(F32)
-        high = lane_roll(low, 64)
-        h_full[cols * s:cols * s + 16, :] = low
-        h_full[cols * s + 16:cols * s + 32, :] = mid
-        h_full[cols * s + 32:cols * s + 48, :] = high
-        square = square + low * low + mid * mid + high * high
+        for k in range(half // 8):
+            low = recv_buf[s, k].astype(F32)
+            high = lane_roll(low, 64)
+            h_full[cols * s + 8 * k:cols * s + 8 * (k + 1), :] = low
+            h_full[cols * s + half + 8 * k:cols * s + half + 8 * (k + 1), :] = high
+            square = square + low * low + high * high
     power = jnp.sum(square, axis=0, keepdims=True)
     inv = lax.rsqrt(power / width + NORM_EPS)
     u_full[...] = (h_full[...] * inv * gain_col[...]).astype(BF16)
@@ -117,18 +124,17 @@
         zj = jnp.transpose(zt_buf[128 * j:128 * (j + 1), :])
         for t in range(ny):
             z_send[t, :, 128 * j:128 * (j + 1)] = zj[rows * t:rows * (t + 1)].astype(BF16)
-    for d in range(1, ny):
-        py = (y + d) % ny
-        remote(z_send.at[py], z_recv.at[y], zsend_sem.at[d], zrecv_sem.at[d], py, x).start()
+    z_sends = [remote(z_send.at[py], z_recv.at[y], zsend_sem.at[d], zrecv_sem.at[d], py, px) for d, py, px in ring(y, mine, ny)]
+    for copy in z_sends:
+        copy.start()
     z_recv[y] = z_send[y]
 
     for j in range(width // 128):
         h_rows[:, 128 * j:128 * (j + 1)] = jnp.transpose(h_full[128 * j:128 * (j + 1), :])
     hrow_ref[...] = h_rows[pl.ds(pl.multiple_of(y * rows, rows), rows), :]
 
-    for d in range(1, ny):
-        py = (y + d) % ny
-        remote(z_send.at[py], z_recv.at[y], zsend_sem.at[d], zrecv_sem.at[d], py, x).wait()
+    for copy in z_sends:
+        copy.wait()
 
     zs = [[z_recv[t, :, 128 * j:128 * (j + 1)].astype(F32) for j in range(w_vmem.shape[0] // 128)] for t in range(ny)]
     for g in range(ny * qcols // 128):
@@ -152,7 +158,7 @@
 def attend_kernel(heads, scale, len_ref, z_ref, k_in, v_in, k_hbm, v_hbm, o_ref, k_ref, v_ref, s_buf, o_acc, k_sem, v_sem):
     rows, slots = k_ref.shape[:2]
 
-    def place(b, carry):
+    def place(b):
         length = len_ref[b]
         base = pl.multiple_of((length // 16) * 16, 16)
         here = lax.broadcasted_iota(jnp.int32, (16, 128), 0) == length - base
@@ -160,18 +166,12 @@
         v_new = jnp.broadcast_to(z_ref[b, heads + 1:heads + 2, :], (16, 128)).astype(BF16)
         k_ref[b, pl.ds(base, 16), :] = jnp.where(here, k_new, k_ref[b, pl.ds(base, 16), :])
         v_ref[b, pl.ds(base, 16), :] = jnp.where(here, v_new, v_ref[b, pl.ds(base, 16), :])
-        return carry
 
     def k_copy(b):
         return pltpu.make_async_copy(k_ref.at[b], k_hbm.at[b], k_sem.at[b])
 
     def v_copy(b):
         return pltpu.make_async_copy(v_ref.at[b], v_hbm.at[b], v_sem.at[b])
-
-    def leave(b, carry):
-        k_copy(b).start()
-        v_copy(b).start()
-        return carry
 
     def score(i, slot):
         blank = jnp.zeros((16, 128), BF16)
@@ -192,8 +192,12 @@
         o_acc[2 * i] = o[0:16, 0:128]
         o_acc[2 * i + 1] = o[16:32, 128:256]
 
-    lax.fori_loop(0, rows, place, 0)
-    lax.fori_loop(0, rows, leave, 0)
+    for b in range(rows + 1):
+        if b < rows:
+            place(b)
+        if b > 0:
+            k_copy(b - 1).start()
+            v_copy(b - 1).start()
     score(0, 0)
     for i in range(rows // 2 - 1):
         score(i + 1, (i + 1) % 2)
@@ -219,10 +223,10 @@
     heads_y = heads // ny
     many = ny * rows
     ffn = wd_hbm.shape[0]
-    ring = [(d, (y + d) % ny) for d in sorted(range(1, ny), key=lambda d: -min(d, ny - d))]
+    group = ring(y, twist(y, x, ny), ny)
     barrier = pltpu.get_barrier_semaphore()
-    for _, py in ring:
-        pl.semaphore_signal(barrier, inc=1, device_id={'yz': py, 'x': x}, device_id_type=MESH)
+    for _, py, px in group:
+        pl.semaphore_signal(barrier, inc=1, device_id={'yz': py, 'x': px}, device_id_type=MESH)
     wo_copy = pltpu.make_async_copy(wo_hbm, wo, wo_sem)
     gain_copy = pltpu.make_async_copy(gain_hbm, gain_ref, gain_sem)
     parts = wgu_sem.shape[0]
@@ -234,7 +238,7 @@
         copy.start()
     pl.semaphore_wait(barrier, ny - 1)
 
-    o_sends = [remote(o_ref.at[pl.ds(py * heads_y, heads_y)], o_recv.at[y], os_sem.at[d], or_sem.at[d], py, x) for d, py in ring]
+    o_sends = [remote(o_ref.at[pl.ds(py * heads_y, heads_y)], o_recv.at[y], os_sem.at[d], or_sem.at[d], py, px) for d, py, px in group]
     for copy in o_sends:
         copy.start()
     o_recv[y] = o_ref[pl.ds(y * heads_y, heads_y)]
@@ -250,11 +254,11 @@
 
     def p_copies(c):
         at = pl.ds(c * wide, wide)
-        return [remote(p_send.at[py, :, at], p_recv.at[y, :, at], ps_sem.at[c, d], pr_sem.at[c, d], py, x) for d, py in ring]
+        return [remote(p_send.at[py, :, at], p_recv.at[y, :, at], ps_sem.at[c, d], pr_sem.at[c, d], py, px) for d, py, px in group]
 
     def h_copies(c):
         at = pl.ds(c * wide, wide)
-        return [remote(hm_send.at[:, at], hm_recv.at[y, :, at], hs_sem.at[c, d], hr_sem.at[c, d], py, x) for d, py in ring]
+        return [remote(hm_send.at[:, at], hm_recv.at[y, :, at], hs_sem.at[c, d], hr_sem.at[c, d], py, px) for d, py, px in group]
 
     for c in range(halves):
         at = slice(c * wide, (c + 1) * wide)
@@ -351,20 +355,22 @@
 
     sums = [[jnp.zeros((16, 128), F32) for _ in range(3)] for _ in range(ny)]
     olds = [[jnp.zeros((16, 128), F32) for _ in range(3)] for _ in range(ny)]
-    for px in range(nx):
-        mine = (lane16 >= rows * px) & (lane16 < rows * (px + 1))
-        low = f_recv[px, 0:16].astype(F32)
+    for g in range(nx):
+        members = [twist(t, g, ny) for t in range(ny)]
+        low = f_recv[members[0], 0:16].astype(F32)
         for t in range(1, ny):
-            low = low + f_recv[t * nx + px, 0:16].astype(F32)
-        corner = [f_recv[t * nx + px, 16:32].astype(F32) for t in range(ny)]
+            low = low + f_recv[t * nx + members[t], 0:16].astype(F32)
+        corner = [f_recv[t * nx + members[t], 16:32].astype(F32) for t in range(ny)]
         mid = corner[0]
         for t in range(1, ny):
             mid = mid + corner[t]
         high = lane_roll(low, 64)
         for t in range(ny):
+            at = rows * members[t]
+            here = (lane16 >= at) & (lane16 < at + rows)
             for k, v in enumerate((low, mid, high)):
-                sums[t][k] = jnp.where(mine, lane_roll(v, rows * px - rows * t), sums[t][k])
-                olds[t][k] = jnp.where(mine, lane_roll(corner[t], rows * px - 64 - 16 * k), olds[t][k])
+                sums[t][k] = jnp.where(here, lane_roll(v, at - rows * t), sums[t][k])
+                olds[t][k] = jnp.where(here, lane_roll(corner[t], at - 64 - 16 * k), olds[t][k])
     for t in range(ny):
         for k in range(3):
             out_ref[16 * k:16 * (k + 1), 128 * t:128 * (t + 1)] = (olds[t][k] + sums[t][k]).astype(BF16)
@@ -403,7 +409,7 @@
             out_specs=(vmem,) * 4,
             scratch_shapes=[
                 pltpu.VMEM(ht.shape, BF16), pltpu.VMEM(attn_gain.shape, BF16),
-                pltpu.VMEM((nx, 32, 128), BF16), pltpu.VMEM((total, 32, 128), BF16), pltpu.VMEM((qpad, width), BF16),
+                pltpu.VMEM((nx, cols // 16, 8, 128), BF16), pltpu.VMEM((total, cols // 16, 8, 128), BF16), pltpu.VMEM((qpad, width), BF16),
                 pltpu.VMEM((width, 128), F32), pltpu.VMEM((width, 128), F32), pltpu.VMEM((width, 128), BF16),
                 pltpu.VMEM((qpad, 128), F32), pltpu.VMEM((ny, rows, qpad), BF16), pltpu.VMEM((ny, rows, qpad), BF16),
                 pltpu.VMEM((128, width), F32),

time: 55 us -> 54.4 us (0.989)
  Pallas kernels: 53.6 us -> 52.9 us
    pallas_call x1, Pallas kernels: 16.1 us -> 13.5 us  [layer(): pl.pallas_call(functools.partial(mlp_kernel, ny, nx, cols, rows, width, f...]
    pallas_call x1, Pallas kernels: 11.6 us -> 13.6 us  [layer(): pl.pallas_call(functools.partial(proj_kernel, ny, nx, cols, rows, width,...]
where the time goes in v5:
time: 54.4 us; the launch traced here: 54.2 us
  Pallas kernels  52.9 us (97%)
  between operations  0.68 us (1%)
  local copies, waits for them, and re-layouts  0.63 us (1%)
    pallas_call x1, Pallas kernels, layer(): pl.pallas_call(functools.partial(qkv_kernel, ny, nx, cols, rows, width),...  19.1 us
    pallas_call x1, Pallas kernels, layer(): pl.pallas_call(functools.partial(proj_kernel, ny, nx, cols, rows, width,...  13.6 us
    pallas_call x1, Pallas kernels, layer(): pl.pallas_call(functools.partial(mlp_kernel, ny, nx, cols, rows, width, f...  13.5 us
    pallas_call x1, Pallas kernels, layer(): pl.pallas_call(functools.partial(attend_kernel, heads, head_dim ** (-0.5)...  6.64 us

profile of v5, /device:TPU:97, one launch (start us, length us, event | category | flops | bytes accessed | tf_op | source)
XLA Modules:
  0.0 54.2 jit_solution(1800485852965339957)
XLA Ops:
  0.6 0.0 copy-start
  0.6 19.1 %qkv.1 = (f32[16,16,128]{2,1,0:T(8,128)S(1)}, f32[16,1536]{1,0:T(8,128)S(1)}, bf16[16,2048,128]{2,1,0:T(8,128)(2,1)S(1)}, bf16[16,2048,128]{2,1,0:T(8,128)(2,1)S(1)}) custom-call(bf16[48,512]{1,0:T(8,128)(2,1)} %bitcast.21, bf16[1,1536]{1,0:T(2,128)(2,1)} %gain_hbm.2, bf16[448,1536]{1,0:T(8,128)(2,1)} %bitcast.19, bf16[16,2048,128]{2,1,0:T(8,128)(2,1)} %bitcast.16, ...), custom_call_target="tpu_custom_call" | custom-call | flops 8000000000 | bytes 20000000 | tf_op jit(solution)/shard_map/qkv/pallas_call | solution.py:404
  19.8 0.0 copy-done
  19.8 6.6 %attend.1 = (bf16[16,2048,128]{2,1,0:T(8,128)(2,1)}, bf16[16,2048,128]{2,1,0:T(8,128)(2,1)}, bf16[12,16,128]{2,1,0:T(8,128)(2,1)S(1)}, bf16[16,2048,128]{2,1,0:T(8,128)(2,1)S(1)}, bf16[16,2048,128]{2,1,0:T(8,128)(2,1)S(1)}) custom-call(s32[16]{0:T(128)S(1)} %copy-done, ...), custom_call_target="tpu_custom_call", output_to_operand_aliasing={{3}: (2, {}), {4}: (3, {})} | custom-call | flops 8000000000 | bytes 20000000 | tf_op jit(solution)/shard_map/attend/pallas_call | solution.py:421
  26.5 13.6 %proj.1 = (bf16[128,1536]{1,0:T(8,128)(2,1)S(1)}, f32[32,16,128]{2,1,0:T(8,128)S(1)}, bf16[2,2240,1536]{2,1,0:T(8,128)(2,1)S(1)}, bf16[2304,1536]{1,0:T(8,128)(2,1)S(1)}) custom-call(bf16[12,16,128]{2,1,0:T(8,128)(2,1)S(1)} %get-tuple-element.17.o_ref, f32[16,1536]{1,0:T(8,128)S(1)} %get-tuple-element.18.hrow_ref, bf16[1,1536]{1,0:T(2,128)(2,1)} %gain_hbm.3, ...), custom_call_target="tpu_custom_call" | custom-call | flops 8000000000 | bytes 20000000 | tf_op jit(solution)/shard_map/proj/pallas_call | solution.py:434
  40.1 13.5 %mlp.1 = bf16[48,512]{1,0:T(8,128)(2,1)S(1)} custom-call(bf16[128,1536]{1,0:T(8,128)(2,1)S(1)} %get-tuple-element.19.u_ref, f32[32,16,128]{2,1,0:T(8,128)S(1)} %get-tuple-element.20.tail_ref, bf16[2,2240,1536]{2,1,0:T(8,128)(2,1)S(1)} %get-tuple-element.21.wgu, bf16[2304,1536]{1,0:T(8,128)(2,1)S(1)} %get-tuple-element.22.wd), custom_call_target="tpu_custom_call" | custom-call | flops 8000000000 | bytes 20000000 | tf_op jit(solution)/shard_map/mlp/pallas_call | solution.py:452
  53.6 0.6 %copy.18 = bf16[512,48]{0,1:T(8,128)(2,1)} copy(bf16[512,48]{0,1:T(8,128)(2,1)S(1)} %bitcast.14) | data formatting | bytes 98304
Async XLA Ops:
  0.6 19.2 %copy-start = (s32[16]{0:T(128)S(1)}, s32[16]{0:T(128)}, u32[]{:S(2)}) copy-start(s32[16]{0:T(128)} %len_ref.1) | copy-start | bytes 196

commit v6 on v5

--- a/solution.py
+++ b/solution.py
@@ -136,34 +136,40 @@
     for copy in z_sends:
         copy.wait()
 
-    zs = [[z_recv[t, :, 128 * j:128 * (j + 1)].astype(F32) for j in range(w_vmem.shape[0] // 128)] for t in range(ny)]
-    for g in range(ny * qcols // 128):
-        start = 128 * g
-        t = start // qcols
-        off = start - t * qcols
+    z_ref[...] = z_recv[...]
+    for copy in kv_copies:
+        copy.wait()
+
+
+def attend_kernel(heads, qcols, scale, len_ref, z_recv, k_in, v_in, k_hbm, v_hbm, o_ref, k_ref, v_ref, z_ref, new_rows, s_buf, o_acc, k_sem, v_sem):
+    rows, slots = k_ref.shape[:2]
+    ny = z_recv.shape[0]
+    lane16 = lane_ids((16, 128))
+
+    def column(g):
+        t, off = 128 * g // qcols, 128 * g % qcols
         j, sh = off // 128, off % 128
         take = min(128, qcols - off)
-        out = lane_roll(zs[t][j], -sh)
+
+        def tile(t, j):
+            return z_recv[t, :, 128 * j:128 * (j + 1)].astype(F32)
+
+        out = lane_roll(tile(t, j), -sh)
         if sh and take > 128 - sh:
-            out = jnp.where(lane16 < 128 - sh, out, lane_roll(zs[t][j + 1], -sh))
+            out = jnp.where(lane16 < 128 - sh, out, lane_roll(tile(t, j + 1), -sh))
         if take < 128:
-            out = jnp.where(lane16 < take, out, lane_roll(zs[t + 1][0], take))
-        z_ref[:, g, :] = out
-    for g in range(ny * qcols // 128, z_ref.shape[1]):
-        z_ref[:, g, :] = jnp.zeros((rows, 128), F32)
-    for copy in kv_copies:
-        copy.wait()
-
-
-def attend_kernel(heads, scale, len_ref, z_ref, k_in, v_in, k_hbm, v_hbm, o_ref, k_ref, v_ref, s_buf, o_acc, k_sem, v_sem):
-    rows, slots = k_ref.shape[:2]
+            out = jnp.where(lane16 < take, out, lane_roll(tile(t + 1, 0), take))
+        return out
+
+    new_rows[0] = column(heads)
+    new_rows[1] = column(heads + 1)
 
     def place(b):
         length = len_ref[b]
         base = pl.multiple_of((length // 16) * 16, 16)
         here = lax.broadcasted_iota(jnp.int32, (16, 128), 0) == length - base
-        k_new = jnp.broadcast_to(z_ref[b, heads:heads + 1, :], (16, 128)).astype(BF16)
-        v_new = jnp.broadcast_to(z_ref[b, heads + 1:heads + 2, :], (16, 128)).astype(BF16)
+        k_new = jnp.broadcast_to(new_rows[0, pl.ds(b, 1), :], (16, 128)).astype(BF16)
+        v_new = jnp.broadcast_to(new_rows[1, pl.ds(b, 1), :], (16, 128)).astype(BF16)
         k_ref[b, pl.ds(base, 16), :] = jnp.where(here, k_new, k_ref[b, pl.ds(base, 16), :])
         v_ref[b, pl.ds(base, 16), :] = jnp.where(here, v_new, v_ref[b, pl.ds(base, 16), :])
 
@@ -192,12 +198,26 @@
         o_acc[2 * i] = o[0:16, 0:128]
         o_acc[2 * i + 1] = o[16:32, 128:256]
 
-    for b in range(rows + 1):
-        if b < rows:
-            place(b)
-        if b > 0:
-            k_copy(b - 1).start()
-            v_copy(b - 1).start()
+    def leave(b, carry):
+        k_copy(b).start()
+        v_copy(b).start()
+        return carry
+
+    def enter(i, carry):
+        place(2 * i)
+        place(2 * i + 1)
+        leave(2 * i - 2, 0)
+        leave(2 * i - 1, 0)
+        return carry
+
+    place(0)
+    place(1)
+    lax.fori_loop(1, rows // 2, enter, 0)
+    lax.fori_loop(rows - 2, rows, leave, 0)
+    for h in range(heads):
+        z_ref[:, h, :] = column(h)
+    for h in range(heads, 16):
+        z_ref[:, h, :] = jnp.zeros((rows, 128), F32)
     score(0, 0)
     for i in range(rows // 2 - 1):
         score(i + 1, (i + 1) % 2)
@@ -323,28 +343,43 @@
         for j in range(m.shape[0] // 128):
             m_rows[:, base + 128 * j:base + 128 * (j + 1)] = jnp.transpose(m[128 * j:128 * (j + 1)])[0:many].astype(BF16)
 
-    chunks = f_part.shape[0]
+    chunks = f_cols.shape[0]
     wide = width // chunks
     group = total // chunks
     span = nx // chunks
-    own = (x % span) * ny + y
-    f_part[:, many:, :] = jnp.zeros((chunks, f_part.shape[1] - many, wide), F32)
+    f_cols[:, :, many:] = jnp.zeros((chunks, wide, 128 - many), F32)
     pl.semaphore_wait(barrier, total - 1)
     f_sends = []
-    for i in range(chunks):
+    def product(i):
         c = (x // span + 1 + i) % chunks
         at = pl.ds(pl.multiple_of(c * wide, wide), wide)
-        f_part[i, 0:many, :] = lax.dot_general(m_rows[...], wd[:, at], NN, preferred_element_type=F32)
+        f_part[i] = lax.dot_general(m_rows[...], wd[:, at], NN, preferred_element_type=F32)
+
+    def pack(i):
+        c = (x // span + 1 + i) % chunks
         for j in range(wide // 128):
-            f_cols[i, 128 * j:128 * (j + 1), :] = jnp.transpose(f_part[i, :, 128 * j:128 * (j + 1)])
+            f_cols[i, 128 * j:128 * (j + 1), 0:many] = jnp.transpose(f_part[i, :, 128 * j:128 * (j + 1)])
         for s in range(group):
             a0 = f_cols[i, cols * s:cols * s + 16, :]
             a1 = f_cols[i, cols * s + 16:cols * s + 32, :]
             a2 = lane_roll(f_cols[i, cols * s + 32:cols * s + 48, :], 64)
             f_send[c * group + s, 0:16] = jnp.where(lane16 < 64, a0, a2).astype(BF16)
             f_send[c * group + s, 16:32] = jnp.where(lane16 < 64, a1, tail_ref[c * group + s]).astype(BF16)
-        for k in range(1 if i == chunks - 1 else 0, group):
-            j = (own + k) % group
+
+    product(0)
+    for i in range(chunks):
+        pack(i)
+        if i + 1 < chunks:
+            product(i + 1)
+        c = (x // span + 1 + i) % chunks
+        last = i == chunks - 1
+        order = [((x + (2 if last else 0)) // 2 * 2 + p) % span for p in range(2)]
+        order += [((x + (0 if last else 2)) // 2 * 2 + p) % span for p in range(2)]
+        places = [(px, (y + d) % ny) for px in order for d in (2, 1, 3, 0)]
+        if last:
+            places = places[:8] + [((x + 1 - 2 * (x % 2)) % span, (y + d) % ny) for d in (2, 1, 3, 0)] + [(x % span, (y + d) % ny) for d in (2, 1, 3)]
+        for qx, qy in places:
+            j = qx * ny + qy
             s = c * group + j
             f_sends.append(remote(f_send.at[s], f_recv.at[slot], fs_sem.at[s], fr_sem.at[slot], j % ny, c * span + j // ny))
             f_sends[-1].start()
@@ -403,7 +438,7 @@
         parts = 4
         z, hrow, k_vmem, v_vmem = pl.pallas_call(
             functools.partial(qkv_kernel, ny, nx, cols, rows, width),
-            out_shape=(jax.ShapeDtypeStruct((rows, 16, head_dim), F32), jax.ShapeDtypeStruct((rows, width), F32),
+            out_shape=(jax.ShapeDtypeStruct((ny, rows, qpad), BF16), jax.ShapeDtypeStruct((rows, width), F32),
                        pltpu.VMEM(k_cache.shape, BF16), pltpu.VMEM(v_cache.shape, BF16)),
             in_specs=[hbm] * 5,
             out_specs=(vmem,) * 4,
@@ -419,14 +454,14 @@
             name='qkv',
         )(in_hbm(ht), in_hbm(attn_gain), in_hbm(w_qkv), in_hbm(k_cache), in_hbm(v_cache))
         k_new, v_new, o, _, _ = pl.pallas_call(
-            functools.partial(attend_kernel, heads, head_dim ** -0.5),
+            functools.partial(attend_kernel, heads, qcols, head_dim ** -0.5),
             out_shape=(pltpu.HBM(k_cache.shape, BF16), pltpu.HBM(v_cache.shape, BF16),
                        jax.ShapeDtypeStruct((heads, rows, head_dim), BF16),
                        pltpu.VMEM(k_cache.shape, BF16), pltpu.VMEM(v_cache.shape, BF16)),
             in_specs=[pl.BlockSpec(memory_space=pltpu.SMEM), vmem, vmem, vmem],
             out_specs=(hbm, hbm, vmem, vmem, vmem),
             input_output_aliases={2: 3, 3: 4},
-            scratch_shapes=[pltpu.VMEM((2, 32, slots), F32), pltpu.VMEM((rows, 16, head_dim), F32), dma((rows,)), dma((rows,))],
+            scratch_shapes=[pltpu.VMEM((rows, 16, head_dim), F32), pltpu.VMEM((2, rows, head_dim), F32), pltpu.VMEM((2, 32, slots), F32), pltpu.VMEM((rows, 16, head_dim), F32), dma((rows,)), dma((rows,))],
             compiler_params=pltpu.CompilerParams(vmem_limit_bytes=8 << 20),
             cost_estimate=pl.CostEstimate(flops=8_000_000_000, bytes_accessed=20_000_000, transcendentals=0),
             name='attend',
@@ -455,7 +490,7 @@
             in_specs=[vmem] * 4,
             out_specs=vmem,
             scratch_shapes=[
-                pltpu.VMEM((many, ffn_pad), BF16), pltpu.VMEM((2, 128, width // 2), F32), pltpu.VMEM((2, width // 2, 128), F32),
+                pltpu.VMEM((many, ffn_pad), BF16), pltpu.VMEM((2, many, width // 2), F32), pltpu.VMEM((2, width // 2, 128), F32),
                 pltpu.VMEM((total, 32, 128), BF16), pltpu.VMEM((total, 32, 128), BF16), dma((total,)), dma((total,))],
             compiler_params=pltpu.CompilerParams(collective_id=2, has_side_effects=True, vmem_limit_bytes=12 << 20),
             cost_estimate=pl.CostEstimate(flops=8_000_000_000, bytes_accessed=20_000_000, transcendentals=0),

time: 54.4 us -> 54.4 us (level)
  no operation moved by 1% of the time
where the time goes in v6:
time: 54.4 us; the launch traced here: 54.3 us
  Pallas kernels  53 us (97%)
  between operations  0.68 us (1%)
  local copies, waits for them, and re-layouts  0.63 us (1%)
    pallas_call x1, Pallas kernels, layer(): pl.pallas_call(functools.partial(qkv_kernel, ny, nx, cols, rows, width),...  19 us
    pallas_call x1, Pallas kernels, layer(): pl.pallas_call(functools.partial(proj_kernel, ny, nx, cols, rows, width,...  13.6 us
    pallas_call x1, Pallas kernels, layer(): pl.pallas_call(functools.partial(mlp_kernel, ny, nx, cols, rows, width, f...  13.6 us
    pallas_call x1, Pallas kernels, layer(): pl.pallas_call(functools.partial(attend_kernel, heads, qcols, head_dim **...  6.72 us

profile of v6, /device:TPU:97, one launch (start us, length us, event | category | flops | bytes accessed | tf_op | source)
XLA Modules:
  0.0 54.3 jit_solution(16929202307048064605)
XLA Ops:
  0.6 0.0 copy-start
  0.6 19.0 %qkv.1 = (bf16[4,16,512]{2,1,0:T(8,128)(2,1)S(1)}, f32[16,1536]{1,0:T(8,128)S(1)}, bf16[16,2048,128]{2,1,0:T(8,128)(2,1)S(1)}, bf16[16,2048,128]{2,1,0:T(8,128)(2,1)S(1)}) custom-call(bf16[48,512]{1,0:T(8,128)(2,1)} %bitcast.21, bf16[1,1536]{1,0:T(2,128)(2,1)} %gain_hbm.2, bf16[448,1536]{1,0:T(8,128)(2,1)} %bitcast.19, bf16[16,2048,128]{2,1,0:T(8,128)(2,1)} %bitcast.16, ...), custom_call_target="tpu_custom_call" | custom-call | flops 8000000000 | bytes 20000000 | tf_op jit(solution)/shard_map/qkv/pallas_call | solution.py:439
  19.7 0.0 copy-done
  19.7 6.7 %attend.1 = (bf16[16,2048,128]{2,1,0:T(8,128)(2,1)}, bf16[16,2048,128]{2,1,0:T(8,128)(2,1)}, bf16[12,16,128]{2,1,0:T(8,128)(2,1)S(1)}, bf16[16,2048,128]{2,1,0:T(8,128)(2,1)S(1)}, bf16[16,2048,128]{2,1,0:T(8,128)(2,1)S(1)}) custom-call(s32[16]{0:T(128)S(1)} %copy-done, ...), custom_call_target="tpu_custom_call", output_to_operand_aliasing={{3}: (2, {}), {4}: (3, {})} | custom-call | flops 8000000000 | bytes 20000000 | tf_op jit(solution)/shard_map/attend/pallas_call | solution.py:456
  26.4 13.6 %proj.1 = (bf16[128,1536]{1,0:T(8,128)(2,1)S(1)}, f32[32,16,128]{2,1,0:T(8,128)S(1)}, bf16[2,2240,1536]{2,1,0:T(8,128)(2,1)S(1)}, bf16[2304,1536]{1,0:T(8,128)(2,1)S(1)}) custom-call(bf16[12,16,128]{2,1,0:T(8,128)(2,1)S(1)} %get-tuple-element.17.o_ref, f32[16,1536]{1,0:T(8,128)S(1)} %get-tuple-element.18.hrow_ref, bf16[1,1536]{1,0:T(2,128)(2,1)} %gain_hbm.3, ...), custom_call_target="tpu_custom_call" | custom-call | flops 8000000000 | bytes 20000000 | tf_op jit(solution)/shard_map/proj/pallas_call | solution.py:469
  40.0 13.6 %mlp.1 = bf16[48,512]{1,0:T(8,128)(2,1)S(1)} custom-call(bf16[128,1536]{1,0:T(8,128)(2,1)S(1)} %get-tuple-element.19.u_ref, f32[32,16,128]{2,1,0:T(8,128)S(1)} %get-tuple-element.20.tail_ref, bf16[2,2240,1536]{2,1,0:T(8,128)(2,1)S(1)} %get-tuple-element.21.wgu, bf16[2304,1536]{1,0:T(8,128)(2,1)S(1)} %get-tuple-element.22.wd), custom_call_target="tpu_custom_call" | custom-call | flops 8000000000 | bytes 20000000 | tf_op jit(solution)/shard_map/mlp/pallas_call | solution.py:487
  53.7 0.6 %copy.18 = bf16[512,48]{0,1:T(8,128)(2,1)} copy(bf16[512,48]{0,1:T(8,128)(2,1)S(1)} %bitcast.14) | data formatting | bytes 98304
Async XLA Ops:
  0.6 19.0 %copy-start = (s32[16]{0:T(128)S(1)}, s32[16]{0:T(128)}, u32[]{:S(2)}) copy-start(s32[16]{0:T(128)} %len_ref.1) | copy-start | bytes 196

commit v7 on v6

--- a/solution.py
+++ b/solution.py
@@ -24,11 +24,6 @@
     return v if shift == 0 else pltpu.roll(v, shift, v.ndim - 1)
 
 
-def twist(t, g, ny):
-    flip = (t // (ny // 2)) % 2
-    return g + flip * (1 - 2 * (g % 2))
-
-
 def peers(y, x, ny, nx):
     ys = [(y + d) % ny for d in range(ny)]
     xs = [(x + d) % nx for d in range(nx)]
@@ -37,9 +32,9 @@
     return [(dy * nx + dx, ys[dy], xs[dx]) for dx in far_x for dy in far_y if dy or dx]
 
 
-def ring(y, g, ny):
+def ring(y, x, ny):
     far = sorted(range(1, ny), key=lambda d: -min(d, ny - d))
-    return [(d, (y + d) % ny, twist((y + d) % ny, g, ny)) for d in far]
+    return [(d, (y + d) % ny, x) for d in far]
 
 
 def greet_all(others):
@@ -54,11 +49,10 @@
                                         device_id={'yz': py, 'x': px}, device_id_type=MESH)
 
 
-def qkv_kernel(ny, nx, cols, rows, width, ht_hbm, gain_hbm, w_hbm, k_hbm, v_hbm, z_ref, hrow_ref, k_ref, v_ref,
+def qkv_kernel(ny, nx, cols, rows, width, len_hbm, ht_hbm, gain_hbm, w_hbm, k_hbm, v_hbm, z_ref, hrow_ref, k_ref, v_ref, len_ref,
                ht_ref, gain_ref, send_buf, recv_buf, w_vmem, gain_col, h_full, u_full, zt_buf, z_send, z_recv, h_rows,
-               h_sem, g_sem, w_sem, kv_sem, send_sem, recv_sem, zsend_sem, zrecv_sem):
+               len_sem, h_sem, g_sem, w_sem, kv_sem, send_sem, recv_sem, zsend_sem, zrecv_sem):
     y, x = lax.axis_index('yz'), lax.axis_index('x')
-    mine = twist(y, x, ny)
     total = ny * nx
     me = x * ny + y
     qcols = w_hbm.shape[0]
@@ -68,6 +62,8 @@
     barrier = greet_all(others)
     g_copy = pltpu.make_async_copy(gain_hbm, gain_ref, g_sem)
     g_copy.start()
+    len_copy = pltpu.make_async_copy(len_hbm, len_ref, len_sem)
+    len_copy.start()
     w_copy = pltpu.make_async_copy(w_hbm, w_vmem.at[pl.ds(0, qcols)], w_sem)
     w_copy.start()
     parts = kv_sem.shape[1]
@@ -85,7 +81,7 @@
     for g in range(nx):
         block = jnp.zeros((cols, 128), F32)
         for t in range(ny):
-            piece = lane_roll(tiles[t], rows * t - rows * twist(t, g, ny))
+            piece = lane_roll(tiles[t], rows * t - rows * g)
             block = jnp.where((lane >= rows * t) & (lane < rows * (t + 1)), piece, block)
         block = jnp.where(lane[0:half] < 64, block[0:half], lane_roll(block[half:cols], 64))
         for k in range(half // 8):
@@ -93,10 +89,10 @@
 
     pl.semaphore_wait(barrier, total - 1)
 
-    h_sends = [remote(send_buf.at[twist(py, px, ny)], recv_buf.at[me], send_sem.at[d], recv_sem.at[d], py, px) for d, py, px in others]
+    h_sends = [remote(send_buf.at[px], recv_buf.at[me], send_sem.at[d], recv_sem.at[d], py, px) for d, py, px in others]
     for copy in h_sends:
         copy.start()
-    recv_buf[me] = send_buf[mine]
+    recv_buf[me] = send_buf[x]
 
     g_copy.wait()
     for j in range(width // 128):
@@ -124,7 +120,7 @@
         zj = jnp.transpose(zt_buf[128 * j:128 * (j + 1), :])
         for t in range(ny):
             z_send[t, :, 128 * j:128 * (j + 1)] = zj[rows * t:rows * (t + 1)].astype(BF16)
-    z_sends = [remote(z_send.at[py], z_recv.at[y], zsend_sem.at[d], zrecv_sem.at[d], py, px) for d, py, px in ring(y, mine, ny)]
+    z_sends = [remote(z_send.at[py], z_recv.at[y], zsend_sem.at[d], zrecv_sem.at[d], py, px) for d, py, px in ring(y, x, ny)]
     for copy in z_sends:
         copy.start()
     z_recv[y] = z_send[y]
@@ -137,7 +133,7 @@
         copy.wait()
 
     z_ref[...] = z_recv[...]
-    for copy in kv_copies:
+    for copy in kv_copies + [len_copy]:
         copy.wait()
 
 
@@ -243,7 +239,7 @@
     heads_y = heads // ny
     many = ny * rows
     ffn = wd_hbm.shape[0]
-    group = ring(y, twist(y, x, ny), ny)
+    group = ring(y, x, ny)
     barrier = pltpu.get_barrier_semaphore()
     for _, py, px in group:
         pl.semaphore_signal(barrier, inc=1, device_id={'yz': py, 'x': px}, device_id_type=MESH)
@@ -348,7 +344,6 @@
     group = total // chunks
     span = nx // chunks
     f_cols[:, :, many:] = jnp.zeros((chunks, wide, 128 - many), F32)
-    pl.semaphore_wait(barrier, total - 1)
     f_sends = []
     def product(i):
         c = (x // span + 1 + i) % chunks
@@ -371,6 +366,8 @@
         pack(i)
         if i + 1 < chunks:
             product(i + 1)
+        if i == 0:
+            pl.semaphore_wait(barrier, total - 1)
         c = (x // span + 1 + i) % chunks
         last = i == chunks - 1
         order = [((x + (2 if last else 0)) // 2 * 2 + p) % span for p in range(2)]
@@ -391,18 +388,17 @@
     sums = [[jnp.zeros((16, 128), F32) for _ in range(3)] for _ in range(ny)]
     olds = [[jnp.zeros((16, 128), F32) for _ in range(3)] for _ in range(ny)]
     for g in range(nx):
-        members = [twist(t, g, ny) for t in range(ny)]
-        low = f_recv[members[0], 0:16].astype(F32)
+        low = f_recv[g, 0:16].astype(F32)
         for t in range(1, ny):
-            low = low + f_recv[t * nx + members[t], 0:16].astype(F32)
-        corner = [f_recv[t * nx + members[t], 16:32].astype(F32) for t in range(ny)]
+            low = low + f_recv[t * nx + g, 0:16].astype(F32)
+        corner = [f_recv[t * nx + g, 16:32].astype(F32) for t in range(ny)]
         mid = corner[0]
         for t in range(1, ny):
             mid = mid + corner[t]
         high = lane_roll(low, 64)
+        at = rows * g
+        here = (lane16 >= at) & (lane16 < at + rows)
         for t in range(ny):
-            at = rows * members[t]
-            here = (lane16 >= at) & (lane16 < at + rows)
             for k, v in enumerate((low, mid, high)):
                 sums[t][k] = jnp.where(here, lane_roll(v, at - rows * t), sums[t][k])
                 olds[t][k] = jnp.where(here, lane_roll(corner[t], at - 64 - 16 * k), olds[t][k])
@@ -436,23 +432,23 @@
         ffn_pad = -(-ffn // 128) * 128
         in_hbm = functools.partial(pltpu.with_memory_space_constraint, memory_space=pltpu.HBM)
         parts = 4
-        z, hrow, k_vmem, v_vmem = pl.pallas_call(
+        z, hrow, k_vmem, v_vmem, lens = pl.pallas_call(
             functools.partial(qkv_kernel, ny, nx, cols, rows, width),
             out_shape=(jax.ShapeDtypeStruct((ny, rows, qpad), BF16), jax.ShapeDtypeStruct((rows, width), F32),
-                       pltpu.VMEM(k_cache.shape, BF16), pltpu.VMEM(v_cache.shape, BF16)),
-            in_specs=[hbm] * 5,
-            out_specs=(vmem,) * 4,
+                       pltpu.VMEM(k_cache.shape, BF16), pltpu.VMEM(v_cache.shape, BF16), pltpu.SMEM((rows,), jnp.int32)),
+            in_specs=[hbm] * 6,
+            out_specs=(vmem,) * 4 + (pl.BlockSpec(memory_space=pltpu.SMEM),),
             scratch_shapes=[
                 pltpu.VMEM(ht.shape, BF16), pltpu.VMEM(attn_gain.shape, BF16),
                 pltpu.VMEM((nx, cols // 16, 8, 128), BF16), pltpu.VMEM((total, cols // 16, 8, 128), BF16), pltpu.VMEM((qpad, width), BF16),
                 pltpu.VMEM((width, 128), F32), pltpu.VMEM((width, 128), F32), pltpu.VMEM((width, 128), BF16),
                 pltpu.VMEM((qpad, 128), F32), pltpu.VMEM((ny, rows, qpad), BF16), pltpu.VMEM((ny, rows, qpad), BF16),
                 pltpu.VMEM((128, width), F32),
-                dma, dma, dma, dma((2, parts)), dma((total,)), dma((total,)), dma((ny,)), dma((ny,))],
+                dma, dma, dma, dma, dma((2, parts)), dma((total,)), dma((total,)), dma((ny,)), dma((ny,))],
             compiler_params=pltpu.CompilerParams(collective_id=0, has_side_effects=True, vmem_limit_bytes=12 << 20),
             cost_estimate=pl.CostEstimate(flops=8_000_000_000, bytes_accessed=20_000_000, transcendentals=0),
             name='qkv',
-        )(in_hbm(ht), in_hbm(attn_gain), in_hbm(w_qkv), in_hbm(k_cache), in_hbm(v_cache))
+        )(in_hbm(seq_lens), in_hbm(ht), in_hbm(attn_gain), in_hbm(w_qkv), in_hbm(k_cache), in_hbm(v_cache))
         k_new, v_new, o, _, _ = pl.pallas_call(
             functools.partial(attend_kernel, heads, qcols, head_dim ** -0.5),
             out_shape=(pltpu.HBM(k_cache.shape, BF16), pltpu.HBM(v_cache.shape, BF16),
@@ -465,7 +461,7 @@
             compiler_params=pltpu.CompilerParams(vmem_limit_bytes=8 << 20),
             cost_estimate=pl.CostEstimate(flops=8_000_000_000, bytes_accessed=20_000_000, transcendentals=0),
             name='attend',
-        )(seq_lens, z, k_vmem, v_vmem)
+        )(lens, z, k_vmem, v_vmem)
         u, tail, wgu_vmem, wd_vmem = pl.pallas_call(
             functools.partial(proj_kernel, ny, nx, cols, rows, width, heads),
             out_shape=(pltpu.VMEM((128, width), BF16), pltpu.VMEM((total, 16, 128), F32),

time: 54.4 us -> 52.8 us (0.971)
  Pallas kernels: 53 us -> 51.4 us
    pallas_call x1, Pallas kernels: 13.6 us -> 11.6 us  [layer(): pl.pallas_call(functools.partial(proj_kernel, ny, nx, cols, rows, width,...]
    pallas_call x1, Pallas kernels: 13.6 us -> 14.6 us  [layer(): pl.pallas_call(functools.partial(mlp_kernel, ny, nx, cols, rows, width, f...]
where the time goes in v7:
time: 52.8 us; the launch traced here: 52.7 us
  Pallas kernels  51.4 us (97%)
  between operations  0.66 us (1%)
  local copies, waits for them, and re-layouts  0.62 us (1%)
    pallas_call x1, Pallas kernels, layer(): pl.pallas_call(functools.partial(qkv_kernel, ny, nx, cols, rows, width),...  19 us
    pallas_call x1, Pallas kernels, layer(): pl.pallas_call(functools.partial(mlp_kernel, ny, nx, cols, rows, width, f...  14.6 us
    pallas_call x1, Pallas kernels, layer(): pl.pallas_call(functools.partial(proj_kernel, ny, nx, cols, rows, width,...  11.6 us
    pallas_call x1, Pallas kernels, layer(): pl.pallas_call(functools.partial(attend_kernel, heads, qcols, head_dim **...  6.18 us

profile of v7, /device:TPU:97, one launch (start us, length us, event | category | flops | bytes accessed | tf_op | source)
XLA Modules:
  0.0 52.7 jit_solution(11357008495586672833)
XLA Ops:
  0.6 19.0 %qkv.1 = (bf16[4,16,512]{2,1,0:T(8,128)(2,1)S(1)}, f32[16,1536]{1,0:T(8,128)S(1)}, bf16[16,2048,128]{2,1,0:T(8,128)(2,1)S(1)}, bf16[16,2048,128]{2,1,0:T(8,128)(2,1)S(1)}, s32[16]{0:T(128)S(4)}) custom-call(s32[16]{0:T(128)} %len_hbm.1, bf16[48,512]{1,0:T(8,128)(2,1)} %bitcast.21, bf16[1,1536]{1,0:T(2,128)(2,1)} %gain_hbm.2, bf16[448,1536]{1,0:T(8,128)(2,1)} %bitcast.19, ...), custom_call_target="tpu_custom_call" | custom-call | flops 8000000000 | bytes 20000000 | tf_op jit(solution)/shard_map/qkv/pallas_call | solution.py:435
  19.7 6.2 %attend.1 = (bf16[16,2048,128]{2,1,0:T(8,128)(2,1)}, bf16[16,2048,128]{2,1,0:T(8,128)(2,1)}, bf16[12,16,128]{2,1,0:T(8,128)(2,1)S(1)}, bf16[16,2048,128]{2,1,0:T(8,128)(2,1)S(1)}, bf16[16,2048,128]{2,1,0:T(8,128)(2,1)S(1)}) custom-call(s32[16]{0:T(128)S(4)} %get-tuple-element.15.len_ref, ...), custom_call_target="tpu_custom_call", output_to_operand_aliasing={{3}: (2, {}), {4}: (3, {})} | custom-call | flops 8000000000 | bytes 20000000 | tf_op jit(solution)/shard_map/attend/pallas_call | solution.py:452
  25.9 11.6 %proj.1 = (bf16[128,1536]{1,0:T(8,128)(2,1)S(1)}, f32[32,16,128]{2,1,0:T(8,128)S(1)}, bf16[2,2240,1536]{2,1,0:T(8,128)(2,1)S(1)}, bf16[2304,1536]{1,0:T(8,128)(2,1)S(1)}) custom-call(bf16[12,16,128]{2,1,0:T(8,128)(2,1)S(1)} %get-tuple-element.19.o_ref, f32[16,1536]{1,0:T(8,128)S(1)} %get-tuple-element.20.hrow_ref, bf16[1,1536]{1,0:T(2,128)(2,1)} %gain_hbm.3, ...), custom_call_target="tpu_custom_call" | custom-call | flops 8000000000 | bytes 20000000 | tf_op jit(solution)/shard_map/proj/pallas_call | solution.py:465
  37.5 14.6 %mlp.1 = bf16[48,512]{1,0:T(8,128)(2,1)S(1)} custom-call(bf16[128,1536]{1,0:T(8,128)(2,1)S(1)} %get-tuple-element.21.u_ref, f32[32,16,128]{2,1,0:T(8,128)S(1)} %get-tuple-element.22.tail_ref, bf16[2,2240,1536]{2,1,0:T(8,128)(2,1)S(1)} %get-tuple-element.23.wgu, bf16[2304,1536]{1,0:T(8,128)(2,1)S(1)} %get-tuple-element.24.wd), custom_call_target="tpu_custom_call" | custom-call | flops 8000000000 | bytes 20000000 | tf_op jit(solution)/shard_map/mlp/pallas_call | solution.py:483
  52.1 0.6 %copy.18 = bf16[512,48]{0,1:T(8,128)(2,1)} copy(bf16[512,48]{0,1:T(8,128)(2,1)S(1)} %bitcast.14) | data formatting | bytes 98304

commit v8 on v7

--- a/solution.py
+++ b/solution.py
@@ -231,13 +231,12 @@
 
 
 def proj_kernel(ny, nx, cols, rows, width, heads, o_ref, hrow_ref, gain_hbm, wo_hbm, wgu_hbm, wd_hbm,
-                u_ref, tail_ref, wgu_ref, wd_ref,
-                gain_ref, wo, o_recv, p_send, p_recv, hm_send, hm_recv, hm_rows, hm_cols,
+                h_ref, gain_ref, tail_ref, wgu_ref, wd_ref,
+                wo, o_recv, p_send, p_recv, hm_send, hm_recv, hm_rows, hm_cols,
                 gain_sem, wo_sem, wgu_sem, wd_sem, os_sem, or_sem, ps_sem, pr_sem, hs_sem, hr_sem):
     y, x = lax.axis_index('yz'), lax.axis_index('x')
     total = ny * nx
     heads_y = heads // ny
-    many = ny * rows
     ffn = wd_hbm.shape[0]
     group = ring(y, x, ny)
     barrier = pltpu.get_barrier_semaphore()
@@ -306,20 +305,17 @@
         for k in range(cols // 16):
             corner = corner + lane_roll(hm_cols[cols * s + 16 * k:cols * s + 16 * (k + 1), :], 64 + 16 * k)
         tail_ref[s] = corner
-    u_ref[many:, :] = jnp.zeros((u_ref.shape[0] - many, width), BF16)
 
     gain_copy.wait()
     for c in range(halves):
         for copy in h_copies(c):
             copy.wait()
-    h64 = jnp.concatenate([hm_recv[t] for t in range(ny)], axis=0).astype(F32)
-    inv = lax.rsqrt(jnp.sum(h64 * h64, axis=1, keepdims=True) / width + NORM_EPS)
-    u_ref[0:many, :] = (h64 * inv * gain_ref[...].astype(F32)).astype(BF16)
+    h_ref[...] = hm_recv[...]
     for copy in loads:
         copy.wait()
 
 
-def mlp_kernel(ny, nx, cols, rows, width, ffn, u_ref, tail_ref, wgu, wd, out_ref, m_rows, f_part, f_cols, f_send, f_recv, fs_sem, fr_sem):
+def mlp_kernel(ny, nx, cols, rows, width, ffn, h_ref, gain_ref, tail_ref, wgu, wd, out_ref, u_ref, m_rows, f_part, f_cols, f_send, f_recv, fs_sem, fr_sem):
     y, x = lax.axis_index('yz'), lax.axis_index('x')
     total = ny * nx
     me = x * ny + y
@@ -327,6 +323,10 @@
     many = ny * rows
     barrier = greet_all(peers(y, x, ny, nx))
     lane16 = lane_ids((16, 128))
+    h64 = jnp.concatenate([h_ref[t] for t in range(ny)], axis=0).astype(F32)
+    inv = lax.rsqrt(jnp.sum(h64 * h64, axis=1, keepdims=True) / width + NORM_EPS)
+    u_ref[0:many, :] = (h64 * inv * gain_ref[...].astype(F32)).astype(BF16)
+    u_ref[many:, :] = jnp.zeros((u_ref.shape[0] - many, width), BF16)
 
     for base in range(0, ffn, 512):
         size = min(512, ffn - base)
@@ -462,20 +462,20 @@
             cost_estimate=pl.CostEstimate(flops=8_000_000_000, bytes_accessed=20_000_000, transcendentals=0),
             name='attend',
         )(lens, z, k_vmem, v_vmem)
-        u, tail, wgu_vmem, wd_vmem = pl.pallas_call(
+        h_mid, gain, tail, wgu_vmem, wd_vmem = pl.pallas_call(
             functools.partial(proj_kernel, ny, nx, cols, rows, width, heads),
-            out_shape=(pltpu.VMEM((128, width), BF16), pltpu.VMEM((total, 16, 128), F32),
+            out_shape=(pltpu.VMEM((ny, rows, width), BF16), pltpu.VMEM(mlp_gain.shape, BF16), pltpu.VMEM((total, 16, 128), F32),
                        pltpu.VMEM(w_gate_up.shape, BF16), pltpu.VMEM((ffn_pad, width), BF16)),
             in_specs=[vmem, vmem, hbm, hbm, hbm, hbm],
-            out_specs=(vmem,) * 4,
+            out_specs=(vmem,) * 5,
             scratch_shapes=[
-                pltpu.VMEM(mlp_gain.shape, BF16), pltpu.VMEM(w_out.shape, BF16),
+                pltpu.VMEM(w_out.shape, BF16),
                 pltpu.VMEM((ny, heads // ny, rows, head_dim), BF16),
                 pltpu.VMEM((ny, rows, width), BF16), pltpu.VMEM((ny, rows, width), BF16),
                 pltpu.VMEM((rows, width), BF16), pltpu.VMEM((ny, rows, width), BF16),
                 pltpu.VMEM((128, width), F32), pltpu.VMEM((width, 128), F32),
                 dma, dma, dma((5,)), dma, dma((ny,)), dma((ny,)),
-                dma((2, ny)), dma((2, ny)), dma((2, ny)), dma((2, ny))],
+                dma((3, ny)), dma((3, ny)), dma((3, ny)), dma((3, ny))],
             compiler_params=pltpu.CompilerParams(collective_id=1, has_side_effects=True, vmem_limit_bytes=12 << 20),
             cost_estimate=pl.CostEstimate(flops=8_000_000_000, bytes_accessed=20_000_000, transcendentals=0),
             name='proj',
@@ -483,15 +483,15 @@
         out = pl.pallas_call(
             functools.partial(mlp_kernel, ny, nx, cols, rows, width, ffn),
             out_shape=jax.ShapeDtypeStruct(ht.shape, BF16),
-            in_specs=[vmem] * 4,
+            in_specs=[vmem] * 5,
             out_specs=vmem,
             scratch_shapes=[
-                pltpu.VMEM((many, ffn_pad), BF16), pltpu.VMEM((2, many, width // 2), F32), pltpu.VMEM((2, width // 2, 128), F32),
+                pltpu.VMEM((128, width), BF16), pltpu.VMEM((many, ffn_pad), BF16), pltpu.VMEM((2, many, width // 2), F32), pltpu.VMEM((2, width // 2, 128), F32),
                 pltpu.VMEM((total, 32, 128), BF16), pltpu.VMEM((total, 32, 128), BF16), dma((total,)), dma((total,))],
             compiler_params=pltpu.CompilerParams(collective_id=2, has_side_effects=True, vmem_limit_bytes=12 << 20),
             cost_estimate=pl.CostEstimate(flops=8_000_000_000, bytes_accessed=20_000_000, transcendentals=0),
             name='mlp',
-        )(u, tail, wgu_vmem, wd_vmem)
+        )(h_mid, gain, tail, wgu_vmem, wd_vmem)
         return out, k_new, v_new
 
     def local_step(hidden, seq_lens, attn_gain, mlp_gain, w_qkv, w_out, w_gate_up, w_down, k_cache, v_cache):

time: 52.8 us -> 52.7 us (level)
  no operation moved by 1% of the time
where the time goes in v8:
time: 52.7 us; the launch traced here: 52.6 us
  Pallas kernels  51.3 us (97%)
  between operations  0.66 us (1%)
  local copies, waits for them, and re-layouts  0.62 us (1%)
    pallas_call x1, Pallas kernels, layer(): pl.pallas_call(functools.partial(qkv_kernel, ny, nx, cols, rows, width),...  19 us
    pallas_call x1, Pallas kernels, layer(): pl.pallas_call(functools.partial(mlp_kernel, ny, nx, cols, rows, width, f...  14.8 us
    pallas_call x1, Pallas kernels, layer(): pl.pallas_call(functools.partial(proj_kernel, ny, nx, cols, rows, width,...  11.3 us
    pallas_call x1, Pallas kernels, layer(): pl.pallas_call(functools.partial(attend_kernel, heads, qcols, head_dim **...  6.18 us

profile of v8, /device:TPU:97, one launch (start us, length us, event | category | flops | bytes accessed | tf_op | source)
XLA Modules:
  0.0 52.6 jit_solution(16548274456082449133)
XLA Ops:
  0.6 19.0 %qkv.1 = (bf16[4,16,512]{2,1,0:T(8,128)(2,1)S(1)}, f32[16,1536]{1,0:T(8,128)S(1)}, bf16[16,2048,128]{2,1,0:T(8,128)(2,1)S(1)}, bf16[16,2048,128]{2,1,0:T(8,128)(2,1)S(1)}, s32[16]{0:T(128)S(4)}) custom-call(s32[16]{0:T(128)} %len_hbm.1, bf16[48,512]{1,0:T(8,128)(2,1)} %bitcast.21, bf16[1,1536]{1,0:T(2,128)(2,1)} %gain_hbm.2, bf16[448,1536]{1,0:T(8,128)(2,1)} %bitcast.19, ...), custom_call_target="tpu_custom_call" | custom-call | flops 8000000000 | bytes 20000000 | tf_op jit(solution)/shard_map/qkv/pallas_call | solution.py:435
  19.7 6.2 %attend.1 = (bf16[16,2048,128]{2,1,0:T(8,128)(2,1)}, bf16[16,2048,128]{2,1,0:T(8,128)(2,1)}, bf16[12,16,128]{2,1,0:T(8,128)(2,1)S(1)}, bf16[16,2048,128]{2,1,0:T(8,128)(2,1)S(1)}, bf16[16,2048,128]{2,1,0:T(8,128)(2,1)S(1)}) custom-call(s32[16]{0:T(128)S(4)} %get-tuple-element.16.len_ref, ...), custom_call_target="tpu_custom_call", output_to_operand_aliasing={{3}: (2, {}), {4}: (3, {})} | custom-call | flops 8000000000 | bytes 20000000 | tf_op jit(solution)/shard_map/attend/pallas_call | solution.py:452
  25.9 11.3 %proj.1 = (bf16[4,16,1536]{2,1,0:T(8,128)(2,1)S(1)}, bf16[1,1536]{1,0:T(2,128)(2,1)S(1)}, f32[32,16,128]{2,1,0:T(8,128)S(1)}, bf16[2,2240,1536]{2,1,0:T(8,128)(2,1)S(1)}, bf16[2304,1536]{1,0:T(8,128)(2,1)S(1)}) custom-call(bf16[12,16,128]{2,1,0:T(8,128)(2,1)S(1)} %get-tuple-element.20.o_ref, f32[16,1536]{1,0:T(8,128)S(1)} %get-tuple-element.21.hrow_ref, ...), custom_call_target="tpu_custom_call" | custom-call | flops 8000000000 | bytes 20000000 | tf_op jit(solution)/shard_map/proj/pallas_call | solution.py:465
  37.2 14.8 %mlp.1 = bf16[48,512]{1,0:T(8,128)(2,1)S(1)} custom-call(bf16[4,16,1536]{2,1,0:T(8,128)(2,1)S(1)} %get-tuple-element.22.h_ref, bf16[1,1536]{1,0:T(2,128)(2,1)S(1)} %get-tuple-element.23.gain_ref, f32[32,16,128]{2,1,0:T(8,128)S(1)} %get-tuple-element.24.tail_ref, bf16[2,2240,1536]{2,1,0:T(8,128)(2,1)S(1)} %get-tuple-element.25.wgu, ...), custom_call_target="tpu_custom_call" | custom-call | flops 8000000000 | bytes 20000000 | tf_op jit(solution)/shard_map/mlp/pallas_call | solution.py:483
  52.0 0.6 %copy.18 = bf16[512,48]{0,1:T(8,128)(2,1)} copy(bf16[512,48]{0,1:T(8,128)(2,1)S(1)} %bitcast.14) | data formatting | bytes 98304
